TPU v7x, 32 devices: a whole 2x2x4 slice. The times are simulated.
32 devices in a mesh: inner: 4 (over z), outer: 8 (over y, x, core).
Axes of the slice: x: 2, y: 2, z: 4, core: 2. Of those that a mesh axis runs over, the one named last changes fastest.
Arguments:
- inner_state: float32 [2, 16, 2048], P(None, 'inner', 'outer'), may hold values from -6 to 6
- outer_state: float32 [2, 640, 4096], P(None, 'inner', 'outer'), may hold values from -6 to 6
- energies: float32 [16, 2048], P('inner', 'outer'), may hold values from -2 to 2
- dipole: float32 [16, 2048, 2048], P('inner', 'outer'), may hold values from -0.125 to 0.125
- surface: float32 [16, 40, 2048], P('inner', None, 'outer'), may hold values from -0.125 to 0.125
- thresholds: float32 [640], P('inner'), may hold values from 0 to 2
- coupling_coef: float32 [16, 40, 40], P('inner'), may hold values from -1 to 1
- coupling_pattern: int32 [16, 40, 40], P('inner'), may hold values 0 or 1
- block_sizes: int32 [16], P('inner'), may hold values from 1 to 2048, 30720 in all
- field_strength: float32 [2], replicated, may hold values from 0.5 to 2
Outputs:
- inner_final: float32 [2, 16, 2048], P(None, 'inner', 'outer')
- outer_final: float32 [2, 640, 4096], P(None, 'inner', 'outer')
All inputs are finite; a program needn't handle non-finite values. No bound on the sum of `coupling_pattern` or of `block_sizes` on one device may be relied on, other than what follows from the above.
Results may differ from a plain program's by a relative error of at most 0.0001.
Values sent between devices are 32-bit elements; how exact they have to be, the bound alone decides.
A program may use at most 128 MiB of HBM per device.

v0:
```python
import jax
import jax.numpy as jnp
from jax import lax
from jax.sharding import PartitionSpec as P

STEPS = 2
ORDER = 4


kinetic_scale = 3.125
time_step = 0.1


def from_behind(block, axis, distance):
    devices = range(lax.axis_size(axis))
    route = [(i - distance, i) for i in devices if i - distance in devices]
    return lax.ppermute(block, axis, route)


def spread(shard, axis, root):
    mine = lax.axis_index(axis) == root
    return lax.psum(jnp.where(mine, shard, jnp.zeros_like(shard)), axis)


def with_halo(cells, sides, width):
    for axis, dim in sides:
        count = lax.axis_size(axis)
        ends = count - 1
        head = lax.slice_in_dim(cells, 0, width, axis=dim)
        tail = lax.slice_in_dim(cells, cells.shape[dim] - width, cells.shape[dim], axis=dim)
        cells = jnp.concatenate(
            [
                lax.ppermute(tail, axis, [(i, (i + 1) % count) for i in range(ends)]),
                cells,
                lax.ppermute(head, axis, [((i + 1) % count, i) for i in range(ends)]),
            ],
            axis=dim,
        )
    return cells


def reduce_partials(partial_terms, partial_boundary):
    own_terms = lax.psum_scatter(partial_terms, "outer", scatter_dimension=2, tiled=True)
    boundary = lax.psum(partial_boundary, "outer")
    return (own_terms, boundary)


def local(
    inner_state,
    outer_state,
    energies,
    dipole,
    surface,
    thresholds,
    coupling_coef,
    coupling_pattern,
    block_sizes,
    field_strength,
):
    highest = lax.Precision.HIGHEST
    blocks = dipole.shape[0]
    row_count = dipole.shape[1]
    channels = coupling_coef.shape[1]
    radial = outer_state.shape[2]
    sector_index = lax.axis_index("outer")
    row_index = sector_index * row_count + jnp.arange(row_count, dtype=jnp.int32)
    live_rows = (row_index[None, :] < block_sizes[:, None]).astype(jnp.float32)
    coupling = coupling_coef * coupling_pattern.astype(jnp.float32)
    first_sector = jnp.where(sector_index == 0, 1.0, 0.0).astype(jnp.float32)
    edge_mask = first_sector * (jnp.arange(radial, dtype=jnp.int32) == 0).astype(jnp.float32)
    prev_dipole, prev_coupling = from_behind((dipole[blocks - 1], coupling[blocks - 1]), "inner", 1)
    current = (inner_state * live_rows, outer_state)
    for time_index in range(STEPS):
        strength = field_strength[time_index]
        taylor_term = current
        accumulated = current
        for power in range(1, ORDER + 1):
            inner_part = taylor_term[0]
            outer_part = taylor_term[1]
            channel_grid = outer_part.reshape(2, blocks, channels, radial)
            next_first, next_channels = from_behind(
                (inner_part[:, 0], channel_grid[:, 0]), "inner", -1
            )
            extended = jnp.concatenate([inner_part, next_first[:, None]], axis=1)
            gathered = lax.all_gather(extended, "outer", axis=2, tiled=True)
            edge_values = spread(outer_part[:, :, 0], "outer", 0)
            forward = jnp.einsum("lij,plj->pli", dipole, gathered[:, 1:], precision=highest)
            grid_next = jnp.concatenate([channel_grid[:, 1:], next_channels[:, None]], axis=1)
            upward = jnp.einsum("lab,plbr->plar", coupling, grid_next, precision=highest)
            partial_boundary = jnp.einsum("lcs,pls->plc", surface, inner_part, precision=highest)
            prev_rows, prev_channels = from_behind(
                (inner_part[:, blocks - 1], channel_grid[:, blocks - 1]), "inner", 1
            )
            source_rows = jnp.concatenate([prev_rows[:, None], inner_part[:, : blocks - 1]], axis=1)
            source_blocks = jnp.concatenate([prev_dipole[None], dipole[: blocks - 1]], axis=0)
            partial_terms = jnp.einsum(
                "lji,plj->pli", source_blocks, source_rows, precision=highest
            )
            backward, boundary = reduce_partials(partial_terms, partial_boundary)
            source_grid = jnp.concatenate(
                [prev_channels[:, None], channel_grid[:, : blocks - 1]], axis=1
            )
            source_coupling = jnp.concatenate([prev_coupling[None], coupling[: blocks - 1]], axis=0)
            downward = jnp.einsum("lba,plbr->plar", source_coupling, source_grid, precision=highest)
            first_point = edge_values.reshape(2, blocks, channels)
            surf_term = jnp.einsum("lcs,plc->pls", surface, first_point, precision=highest)
            inner_image = live_rows * (
                energies * inner_part + strength * (forward + backward) - kinetic_scale * surf_term
            )
            padded = with_halo(outer_part, (("outer", 2),), 1)
            left_cells = (
                padded[:, :, :radial]
                + edge_mask[None, None, :] * boundary.reshape(2, blocks * channels)[:, :, None]
            )
            right_cells = padded[:, :, 2:]
            kinetic = kinetic_scale * (2.0 * outer_part - left_cells - right_cells)
            outer_image = (
                kinetic
                + thresholds[None, :, None] * outer_part
                + strength * (upward + downward).reshape(2, blocks * channels, radial)
            )
            inner_image, outer_image = (inner_image, outer_image)
            factor = time_step / power
            taylor_term = (
                factor * jnp.stack([inner_image[1], -inner_image[0]]),
                factor * jnp.stack([outer_image[1], -outer_image[0]]),
            )
            accumulated = (accumulated[0] + taylor_term[0], accumulated[1] + taylor_term[1])
        current = accumulated
    return (current[0], current[1])


def solution(mesh):
    placed = (
        P(None, "inner", "outer"),
        P(None, "inner", "outer"),
        P("inner", "outer"),
        P("inner", "outer", None),
        P("inner", None, "outer"),
        P("inner"),
        P("inner", None, None),
        P("inner", None, None),
        P("inner"),
        P(),
    )
    return jax.shard_map(
        local,
        mesh=mesh,
        in_specs=placed,
        out_specs=(P(None, "inner", "outer"), P(None, "inner", "outer")),
        check_vma=False,
    )
```

profile of v0, /device:TPU:0, one launch (start us, length us, event | category | flops | bytes accessed | tf_op | source)
XLA Modules:
  0.0 834.1 jit_solution(18084127534141652575)
XLA Ops:
  8.7 5.0 collective-permute-start.1
  38.6 13.0 %all-reduce.7 = (f32[2,160]{1,0:T(2,128)}, f32[2,4,40]{2,0,1:T(2,128)S(1)}) all-reduce(f32[2,160]{1,0:T(2,128)S(1)} %mul.616, f32[2,4,40]{2,0,1:T(2,128)S(1)} %copy.69), channel_id=1, replica_groups=mesh['inner'=4,'outer'=8] {'outer'}, use_global_device_ids=true, to_apply=%region_3.4 | all-reduce | flops 640 | bytes 5120 | tf_op jit(solution)/shard_map/psum | solution.py:44
  53.0 6.3 slice.446
  60.7 8.6 %all_gather.24 = f32[2,5,2048]{2,0,1:T(2,128)S(1)} all-gather(f32[2,5,256]{2,0,1:T(2,128)S(1)} %pad_maximum_fusion.23), channel_id=1, replica_groups=mesh['inner'=4,'outer'=8] {'outer'}, dimensions={2}, use_global_device_ids=true | all-gather | bytes 92160 | tf_op jit(solution)/shard_map/all_gather | solution.py:85
  80.8 4.5 collective-permute-start.15
  86.6 5.3 collective-permute-start.12
  95.6 7.4 convolution_bitcast_fusion.7
  115.7 33.9 %reduce-scatter.25.cloned.1.call-done = f32[256,8]{1,0:T(8,128)} async-done(((f32[2048,8]{1,0:T(8,128)}), f32[256,8]{1,0:T(8,128)}) %reduce-scatter.25.cloned.1.call-update) | async-done | bytes 8208
  152.8 9.8 %fusion.55 = f32[2,4,256]{2,0,1:T(2,128)S(1)} fusion(f32[2,4,256]{2,0,1:T(2,128)S(1)} %fusion.63, f32[2,4,256]{2,0,1:T(2,128)S(1)} %copy.138, f32[2,5,2048]{2,0,1:T(2,128)S(1)} %all_gather.24, f32[4,256,2048]{2,1,0:T(8,128)} %param.13, f32[2,4,256]{2,0,1:T(2,128)S(1)} %copy-done.49, f32[]{:T(128)} %bitcast, f32[4,256]{1,0:T(4,128)S(1)} %copy-done.53, ...), kind=kOutput, calls=%fused_computation.81 | convolution fusion | flops 50343936 | bytes 8511492 | tf_op jit(solution)/shard_map/lij,plj->pli/dot_general | solution.py:87
  163.0 12.5 %all-reduce.6 = (f32[2,160]{1,0:T(2,128)S(1)}, f32[2,4,40]{2,0,1:T(2,128)S(1)}) all-reduce(f32[2,160]{1,0:T(2,128)S(1)} %mul.639, f32[2,4,40]{2,0,1:T(2,128)S(1)} %copy.79), channel_id=1, replica_groups=mesh['inner'=4,'outer'=8] {'outer'}, use_global_device_ids=true, to_apply=%region_6.7 | all-reduce | flops 640 | bytes 5120 | tf_op jit(solution)/shard_map/psum | solution.py:44
  186.4 5.2 collective-permute-start.21
  196.2 6.8 convolution_bitcast_fusion.6
  210.8 12.4 %all_gather.25 = f32[2,5,2048]{2,0,1:T(2,128)S(1)} all-gather(f32[2,5,256]{2,0,1:T(2,128)S(1)} %pad_maximum_fusion.24), channel_id=1, replica_groups=mesh['inner'=4,'outer'=8] {'outer'}, dimensions={2}, use_global_device_ids=true | all-gather | bytes 92160 | tf_op jit(solution)/shard_map/all_gather | solution.py:85
  223.2 28.1 %reduce-scatter.27.cloned.1.call-done = f32[256,8]{1,0:T(8,128)} async-done(((f32[2048,8]{1,0:T(8,128)}), f32[256,8]{1,0:T(8,128)}) %reduce-scatter.27.cloned.1.call-update) | async-done | bytes 8208
  254.5 9.8 %fusion.50 = f32[2,4,256]{2,0,1:T(2,128)S(1)} fusion(f32[2,4,256]{2,0,1:T(2,128)S(1)} %fusion.62, f32[2,4,256]{2,0,1:T(2,128)S(1)} %copy.140, f32[2,5,2048]{2,0,1:T(2,128)S(1)} %all_gather.25, f32[4,256,2048]{2,1,0:T(8,128)} %param.13, f32[4,256]{1,0:T(4,128)S(1)} %get-tuple-element.129, f32[]{:T(128)} %bitcast, f32[4,256]{1,0:T(4,128)S(1)} %compare_convert_fusion, ...), kind=kOutput, calls=%fused_computation.75 | convolution fusion | flops 50345984 | bytes 8511492 | tf_op jit(solution)/shard_map/lij,plj->pli/dot_general | solution.py:87
  268.1 12.8 %all-reduce.5 = (f32[2,160]{1,0:T(2,128)}, f32[2,4,40]{2,0,1:T(2,128)S(1)}) all-reduce(f32[2,160]{1,0:T(2,128)S(1)} %mul.662, f32[2,4,40]{2,0,1:T(2,128)S(1)} %copy.83), channel_id=1, replica_groups=mesh['inner'=4,'outer'=8] {'outer'}, use_global_device_ids=true, to_apply=%region_9.10 | all-reduce | flops 640 | bytes 5120 | tf_op jit(solution)/shard_map/psum | solution.py:44
  282.4 6.8 convolution_bitcast_fusion.5
  297.1 9.3 %all_gather.26 = f32[2,5,2048]{2,0,1:T(2,128)S(1)} all-gather(f32[2,5,256]{2,0,1:T(2,128)S(1)} %pad_maximum_fusion.25), channel_id=1, replica_groups=mesh['inner'=4,'outer'=8] {'outer'}, dimensions={2}, use_global_device_ids=true | all-gather | bytes 92160 | tf_op jit(solution)/shard_map/all_gather | solution.py:85
  317.2 5.2 collective-permute-start.27
  327.6 7.3 reduce-scatter.29.cloned.1.call-done
  338.2 9.8 %fusion.45 = f32[2,4,256]{2,0,1:T(2,128)S(1)} fusion(f32[2,4,256]{2,0,1:T(2,128)S(1)} %fusion.61, f32[2,4,256]{2,0,1:T(2,128)S(1)} %copy.142, f32[2,5,2048]{2,0,1:T(2,128)S(1)} %all_gather.26, f32[4,256,2048]{2,1,0:T(8,128)} %param.13, f32[4,256]{1,0:T(4,128)S(1)} %get-tuple-element.130, f32[]{:T(128)} %bitcast, f32[4,256]{1,0:T(4,128)S(1)} %compare_convert_fusion, ...), kind=kOutput, calls=%fused_computation.69 | convolution fusion | flops 50345984 | bytes 8511492 | tf_op jit(solution)/shard_map/lij,plj->pli/dot_general | solution.py:87
  351.4 12.7 %all-reduce.4 = (f32[2,160]{1,0:T(2,128)}, f32[2,4,40]{2,0,1:T(2,128)S(1)}) all-reduce(f32[2,160]{1,0:T(2,128)S(1)} %mul.684, f32[2,4,40]{2,0,1:T(2,128)} %copy.87), channel_id=1, replica_groups=mesh['inner'=4,'outer'=8] {'outer'}, use_global_device_ids=true, to_apply=%region_12.13 | all-reduce | flops 640 | bytes 5120 | tf_op jit(solution)/shard_map/psum | solution.py:44
  366.4 6.8 convolution_bitcast_fusion.4
  376.4 4.5 reshape.179
  381.0 8.9 %all_gather.27 = f32[2,5,2048]{2,0,1:T(2,128)S(1)} all-gather(f32[2,5,256]{2,0,1:T(2,128)S(1)} %pad_maximum_fusion.26), channel_id=1, replica_groups=mesh['inner'=4,'outer'=8] {'outer'}, dimensions={2}, use_global_device_ids=true | all-gather | bytes 92160 | tf_op jit(solution)/shard_map/all_gather | solution.py:85
  389.9 28.3 %reduce-scatter.31.cloned.1.call-done = f32[256,8]{1,0:T(8,128)} async-done(((f32[2048,8]{1,0:T(8,128)}), f32[256,8]{1,0:T(8,128)}) %reduce-scatter.31.cloned.1.call-update) | async-done | bytes 8208
  421.5 9.8 %fusion.40 = f32[2,4,256]{2,0,1:T(2,128)S(1)} fusion(f32[2,4,256]{2,0,1:T(2,128)} %fusion.60, f32[2,4,256]{2,0,1:T(2,128)S(1)} %copy.144, f32[2,5,2048]{2,0,1:T(2,128)S(1)} %all_gather.27, f32[4,256,2048]{2,1,0:T(8,128)} %param.13, f32[4,256]{1,0:T(4,128)S(1)} %get-tuple-element.128, f32[]{:T(128)} %bitcast, f32[4,256]{1,0:T(4,128)S(1)} %compare_convert_fusion, ...), kind=kOutput, calls=%fused_computation.63 | convolution fusion | flops 50345984 | bytes 8511492 | tf_op jit(solution)/shard_map/lij,plj->pli/dot_general | solution.py:87
  438.2 6.8 convolution_bitcast_fusion.3
  453.5 9.0 %all_gather.28 = f32[2,5,2048]{2,0,1:T(2,128)S(1)} all-gather(f32[2,5,256]{2,0,1:T(2,128)} %pad_maximum_fusion.27), channel_id=1, replica_groups=mesh['inner'=4,'outer'=8] {'outer'}, dimensions={2}, use_global_device_ids=true | all-gather | bytes 92160 | tf_op jit(solution)/shard_map/all_gather | solution.py:85
  473.7 14.4 %all-reduce.3 = (f32[2,160]{1,0:T(2,128)}, f32[2,4,40]{2,0,1:T(2,128)}) all-reduce(f32[2,160]{1,0:T(2,128)} %mul.704, f32[2,4,40]{2,0,1:T(2,128)S(1)} %copy.91), channel_id=1, replica_groups=mesh['inner'=4,'outer'=8] {'outer'}, use_global_device_ids=true, to_apply=%region_15.16 | all-reduce | flops 640 | bytes 5120 | tf_op jit(solution)/shard_map/psum | solution.py:44
  489.5 5.2 collective-permute-start.33
  503.5 9.8 %fusion.35 = f32[2,4,256]{2,0,1:T(2,128)S(1)} fusion(f32[2,4,256]{2,0,1:T(2,128)} %fusion.59, f32[2,4,256]{2,0,1:T(2,128)} %copy.146, f32[2,5,2048]{2,0,1:T(2,128)S(1)} %all_gather.28, f32[4,256,2048]{2,1,0:T(8,128)} %param.13, f32[2,4,256]{2,0,1:T(2,128)S(1)} %fusion.196, f32[]{:T(128)} %bitcast.65, f32[4,256]{1,0:T(4,128)S(1)} %copy-done.53, ...), kind=kOutput, calls=%fused_computation.57 | convolution fusion | flops 50343936 | bytes 8511492 | tf_op jit(solution)/shard_map/lij,plj->pli/dot_general | solution.py:87
  521.0 6.8 convolution_bitcast_fusion.2
  536.4 11.5 %all_gather.29 = f32[2,5,2048]{2,0,1:T(2,128)S(1)} all-gather(f32[2,5,256]{2,0,1:T(2,128)S(1)} %pad_maximum_fusion.28), channel_id=1, replica_groups=mesh['inner'=4,'outer'=8] {'outer'}, dimensions={2}, use_global_device_ids=true | all-gather | bytes 92160 | tf_op jit(solution)/shard_map/all_gather | solution.py:85
  559.4 14.4 %all-reduce.2 = (f32[2,160]{1,0:T(2,128)}, f32[2,4,40]{2,0,1:T(2,128)}) all-reduce(f32[2,160]{1,0:T(2,128)} %mul.721, f32[2,4,40]{2,0,1:T(2,128)S(1)} %copy.99), channel_id=1, replica_groups=mesh['inner'=4,'outer'=8] {'outer'}, use_global_device_ids=true, to_apply=%region_18.19 | all-reduce | flops 640 | bytes 5120 | tf_op jit(solution)/shard_map/psum | solution.py:44
  575.2 5.4 collective-permute-start.39
  589.0 9.8 %fusion.30 = f32[2,4,256]{2,0,1:T(2,128)S(1)} fusion(f32[2,4,256]{2,0,1:T(2,128)} %fusion.58, f32[2,4,256]{2,0,1:T(2,128)} %copy.148, f32[2,5,2048]{2,0,1:T(2,128)S(1)} %all_gather.29, f32[4,256,2048]{2,1,0:T(8,128)} %param.13, f32[]{:T(128)} %bitcast.65, f32[4,256]{1,0:T(4,128)S(1)} %copy-done.55, f32[4,256]{1,0:T(4,128)S(1)} %compare_convert_fusion, ...), kind=kOutput, calls=%fused_computation.51 | convolution fusion | flops 50345984 | bytes 8511492 | tf_op jit(solution)/shard_map/lij,plj->pli/dot_general | solution.py:87
  606.6 6.8 convolution_bitcast_fusion.1
  621.9 11.1 %all_gather.30 = f32[2,5,2048]{2,0,1:T(2,128)S(1)} all-gather(f32[2,5,256]{2,0,1:T(2,128)S(1)} %pad_maximum_fusion.29), channel_id=1, replica_groups=mesh['inner'=4,'outer'=8] {'outer'}, dimensions={2}, use_global_device_ids=true | all-gather | bytes 92160 | tf_op jit(solution)/shard_map/all_gather | solution.py:85
  633.0 28.8 %reduce-scatter.37.cloned.1.call-done = f32[256,8]{1,0:T(8,128)} async-done(((f32[2048,8]{1,0:T(8,128)}), f32[256,8]{1,0:T(8,128)}) %reduce-scatter.37.cloned.1.call-update) | async-done | bytes 8208
  678.8 13.2 %all-reduce.1 = (f32[2,160]{1,0:T(2,128)}, f32[2,4,40]{2,0,1:T(2,128)}) all-reduce(f32[2,160]{1,0:T(2,128)} %mul.738, f32[2,4,40]{2,0,1:T(2,128)} %copy.103), channel_id=1, replica_groups=mesh['inner'=4,'outer'=8] {'outer'}, use_global_device_ids=true, to_apply=%region_21.22 | all-reduce | flops 640 | bytes 5120 | tf_op jit(solution)/shard_map/psum | solution.py:44
  693.0 9.8 %fusion.25 = f32[2,4,256]{2,0,1:T(2,128)S(1)} fusion(f32[2,4,256]{2,0,1:T(2,128)S(1)} %fusion.57, f32[2,4,256]{2,0,1:T(2,128)} %copy.150, f32[2,5,2048]{2,0,1:T(2,128)S(1)} %all_gather.30, f32[4,256,2048]{2,1,0:T(8,128)} %param.13, f32[]{:T(128)} %bitcast.65, f32[4,256]{1,0:T(4,128)S(1)} %get-tuple-element.130, f32[4,256]{1,0:T(4,128)S(1)} %compare_convert_fusion, ...), kind=kOutput, calls=%fused_computation.45 | convolution fusion | flops 50345984 | bytes 8511492 | tf_op jit(solution)/shard_map/lij,plj->pli/dot_general | solution.py:87
  717.9 6.8 convolution_bitcast_fusion
  727.9 4.6 reshape.187
  733.2 12.1 %all_gather.31 = f32[2,5,2048]{2,0,1:T(2,128)S(1)} all-gather(f32[2,5,256]{2,0,1:T(2,128)S(1)} %pad_maximum_fusion.30), channel_id=1, replica_groups=mesh['inner'=4,'outer'=8] {'outer'}, dimensions={2}, use_global_device_ids=true | all-gather | bytes 92160 | tf_op jit(solution)/shard_map/all_gather | solution.py:85
  745.3 28.8 %reduce-scatter.39.cloned.1.call-done = f32[256,8]{1,0:T(8,128)} async-done(((f32[2048,8]{1,0:T(8,128)}), f32[256,8]{1,0:T(8,128)}) %reduce-scatter.39.cloned.1.call-update) | async-done | bytes 8208
  792.9 15.1 %all-reduce = (f32[2,4,40]{2,0,1:T(2,128)S(1)}, f32[2,160]{1,0:T(2,128)S(1)}) all-reduce(f32[2,4,40]{2,0,1:T(2,128)S(1)} %copy.107, f32[2,160]{1,0:T(2,128)S(1)} %mul.753), channel_id=1, replica_groups=mesh['inner'=4,'outer'=8] {'outer'}, use_global_device_ids=true, to_apply=%region_22.23 | all-reduce | flops 640 | bytes 5120 | tf_op jit(solution)/shard_map/psum | solution.py:22
  808.4 10.4 %fusion.20 = f32[2,4,256]{2,0,1:T(2,128)S(1)} fusion(f32[2,4,256]{2,0,1:T(2,128)S(1)} %fusion.56, f32[2,4,256]{2,0,1:T(2,128)S(1)} %copy.152, f32[2,5,2048]{2,0,1:T(2,128)S(1)} %all_gather.31, f32[4,256,2048]{2,1,0:T(8,128)} %param.13, f32[]{:T(128)} %bitcast.65, f32[4,256]{1,0:T(4,128)S(1)} %get-tuple-element.128, f32[4,256]{1,0:T(4,128)S(1)} %compare_convert_fusion, ...), kind=kOutput, calls=%fused_computation.39 | convolution fusion | flops 50345984 | bytes 8511492 | tf_op jit(solution)/shard_map/lij,plj->pli/dot_general | solution.py:87
  (468 shorter events, 285.4 us)
Async XLA Ops:
  7.2 142.4 %reduce-scatter.25.cloned.1.call-start = ((), (), s32[]{:S(2)}) async-start(), calls=%async_computation.8 | async-start | bytes 1179648
  8.7 86.9 %collective-permute-start.1 = (f32[2,256]{1,0:T(2,128)S(1)}, f32[2,256]{1,0:T(2,128)S(1)}, u32[]{:S(2)}, u32[]{:S(2)}) collective-permute-start(f32[2,256]{1,0:T(2,128)S(1)} %get-tuple-element.127), channel_id=1, source_target_pairs={{0,8},{8,16},{16,24},{1,9},{9,17},{17,25},{2,10},{10,18},{18,26},{... | collective-permute-start | bytes 6152 | tf_op jit(solution)/shard_map/ppermute | solution.py:17
  16.9 78.7 %collective-permute-start.2 = (f32[256,2048]{1,0:T(8,128)}, f32[256,2048]{1,0:T(8,128)S(1)}, u32[]{:S(2)}, u32[]{:S(2)}) collective-permute-start(f32[256,2048]{1,0:T(8,128)} %slice_bitcast_fusion), channel_id=1, source_target_pairs={{0,8},{8,16},{16,24},{1,9},{9,17},{17,25},{2,10},{10,18},{18,26},{... | collective-permute-start | bytes 6291464 | tf_op jit(solution)/shard_map/ppermute | solution.py:17
  20.5 38.9 %collective-permute-start = (f32[2,256]{1,0:T(2,128)S(1)}, f32[2,256]{1,0:T(2,128)S(1)}, u32[]{:S(2)}, u32[]{:S(2)}) collective-permute-start(f32[2,256]{1,0:T(2,128)S(1)} %get-tuple-element.126), channel_id=1, source_target_pairs={{8,0},{16,8},{24,16},{9,1},{17,9},{25,17},{10,2},{18,10},{26,18},{... | collective-permute-start | bytes 6152 | tf_op jit(solution)/shard_map/ppermute | solution.py:17
  24.4 44.9 %collective-permute-start.9 = (f32[40,40]{0,1:T(8,128)}, f32[40,40]{0,1:T(8,128)S(1)}, u32[]{:S(2)}, u32[]{:S(2)}) collective-permute-start(f32[40,40]{0,1:T(8,128)} %slice_bitcast_fusion.17), channel_id=1, source_target_pairs={{0,8},{8,16},{16,24},{1,9},{9,17},{17,25},{2,10},{10,18},{18,26},{... | collective-permute-start | bytes 19208 | tf_op jit(solution)/shard_map/ppermute | solution.py:17
  30.0 41.6 %collective-permute-start.8 = (f32[2,40,512]{2,1,0:T(8,128)S(1)}, f32[2,40,512]{2,1,0:T(8,128)}, u32[]{:S(2)}, u32[]{:S(2)}) collective-permute-start(f32[2,40,512]{2,1,0:T(8,128)S(1)} %get-tuple-element.95), channel_id=1, source_target_pairs={{0,8},{8,16},{16,24},{1,9},{9,17},{17,25},{2,10},{10,18},{18,26},{... | collective-permute-start | bytes 491528 | tf_op jit(solution)/shard_map/ppermute | solution.py:17
  59.4 15.1 %collective-permute-start.7 = (f32[2,40,512]{2,1,0:T(8,128)S(1)}, f32[2,40,512]{2,1,0:T(8,128)S(1)}, u32[]{:S(2)}, u32[]{:S(2)}) collective-permute-start(f32[2,40,512]{2,1,0:T(8,128)S(1)} %get-tuple-element.94), channel_id=1, source_target_pairs={{8,0},{16,8},{24,16},{9,1},{17,9},{25,17},{10,2},{18,10},{26,18},{... | collective-permute-start | bytes 491528 | tf_op jit(solution)/shard_map/ppermute | solution.py:17
  85.3 26.8 %collective-permute-start.14 = (f32[2,40,512]{2,1,0:T(8,128)}, f32[2,40,512]{2,1,0:T(8,128)}, u32[]{:S(2)}, u32[]{:S(2)}) collective-permute-start(f32[2,40,512]{2,1,0:T(8,128)} %get-tuple-element.85), channel_id=1, source_target_pairs={{8,0},{16,8},{24,16},{9,1},{17,9},{25,17},{10,2},{18,10},{26,18},{... | collective-permute-start | bytes 491528 | tf_op jit(solution)/shard_map/ppermute | solution.py:17
  86.6 88.9 %collective-permute-start.12 = (f32[2,160,1]{2,1,0:T(8,128)}, f32[2,160,1]{2,1,0:T(8,128)}, u32[]{:S(2)}, u32[]{:S(2)}) collective-permute-start(f32[2,160,1]{2,1,0:T(8,128)} %get-tuple-element.81), channel_id=1, source_target_pairs={{0,1},{1,2},{2,3},{3,4},{4,5},{5,6},{6,7},{8,9},{9,10},{10,11},{11... | collective-permute-start | bytes 3848 | tf_op jit(solution)/shard_map/ppermute | solution.py:33
  92.8 82.8 %collective-permute-start.13 = (f32[2,160,1]{2,1,0:T(8,128)}, f32[2,160,1]{2,1,0:T(8,128)}, u32[]{:S(2)}, u32[]{:S(2)}) collective-permute-start(f32[2,160,1]{2,1,0:T(8,128)} %get-tuple-element.82), channel_id=1, source_target_pairs={{1,0},{2,1},{3,2},{4,3},{5,4},{6,5},{7,6},{9,8},{10,9},{11,10},{12... | collective-permute-start | bytes 3848 | tf_op jit(solution)/shard_map/ppermute | solution.py:35
  111.9 139.3 %reduce-scatter.27.cloned.1.call-start = ((), (), s32[]{:S(2)}) async-start(), calls=%async_computation.9 | async-start | bytes 1179648
  184.0 26.8 %collective-permute-start.3 = (f32[2,256]{1,0:T(2,128)S(1)}, f32[2,256]{1,0:T(2,128)S(1)}, u32[]{:S(2)}, u32[]{:S(2)}) collective-permute-start(f32[2,256]{1,0:T(2,128)S(1)} %get-tuple-element.122), channel_id=1, source_target_pairs={{8,0},{16,8},{24,16},{9,1},{17,9},{25,17},{10,2},{18,10},{26,18},{... | collective-permute-start | bytes 6152 | tf_op jit(solution)/shard_map/ppermute | solution.py:17
  186.4 120.0 %collective-permute-start.21 = (f32[2,40,512]{2,1,0:T(8,128)}, f32[2,40,512]{2,1,0:T(8,128)}, u32[]{:S(2)}, u32[]{:S(2)}) collective-permute-start(f32[2,40,512]{2,1,0:T(8,128)} %get-tuple-element.77), channel_id=1, source_target_pairs={{0,8},{8,16},{16,24},{1,9},{9,17},{17,25},{2,10},{10,18},{18,26},{... | collective-permute-start | bytes 491528 | tf_op jit(solution)/shard_map/ppermute | solution.py:17
  191.6 116.5 %collective-permute-start.20 = (f32[2,40,512]{2,1,0:T(8,128)}, f32[2,40,512]{2,1,0:T(8,128)}, u32[]{:S(2)}, u32[]{:S(2)}) collective-permute-start(f32[2,40,512]{2,1,0:T(8,128)} %get-tuple-element.76), channel_id=1, source_target_pairs={{8,0},{16,8},{24,16},{9,1},{17,9},{25,17},{10,2},{18,10},{26,18},{... | collective-permute-start | bytes 491528 | tf_op jit(solution)/shard_map/ppermute | solution.py:17
  192.9 117.8 %collective-permute-start.18 = (f32[2,160,1]{2,1,0:T(8,128)}, f32[2,160,1]{2,1,0:T(8,128)}, u32[]{:S(2)}, u32[]{:S(2)}) collective-permute-start(f32[2,160,1]{2,1,0:T(8,128)} %get-tuple-element.72), channel_id=1, source_target_pairs={{0,1},{1,2},{2,3},{3,4},{4,5},{5,6},{6,7},{8,9},{9,10},{10,11},{11... | collective-permute-start | bytes 3848 | tf_op jit(solution)/shard_map/ppermute | solution.py:33
  194.9 115.8 %collective-permute-start.19 = (f32[2,160,1]{2,1,0:T(8,128)}, f32[2,160,1]{2,1,0:T(8,128)}, u32[]{:S(2)}, u32[]{:S(2)}) collective-permute-start(f32[2,160,1]{2,1,0:T(8,128)} %get-tuple-element.73), channel_id=1, source_target_pairs={{1,0},{2,1},{3,2},{4,3},{5,4},{6,5},{7,6},{9,8},{10,9},{11,10},{12... | collective-permute-start | bytes 3848 | tf_op jit(solution)/shard_map/ppermute | solution.py:35
  210.7 124.2 %reduce-scatter.29.cloned.1.call-start = ((), (), s32[]{:S(2)}) async-start(), calls=%async_computation.10 | async-start | bytes 1179648
  264.6 16.5 %collective-permute-start.11 = (f32[2,256]{1,0:T(2,128)S(1)}, f32[2,256]{1,0:T(2,128)S(1)}, u32[]{:S(2)}, u32[]{:S(2)}) collective-permute-start(f32[2,256]{1,0:T(2,128)S(1)} %get-tuple-element.119), channel_id=1, source_target_pairs={{0,8},{8,16},{16,24},{1,9},{9,17},{17,25},{2,10},{10,18},{18,26},{... | collective-permute-start | bytes 6152 | tf_op jit(solution)/shard_map/ppermute | solution.py:17
  297.0 121.2 %reduce-scatter.31.cloned.1.call-start = ((), (), s32[]{:S(2)}) async-start(), calls=%async_computation.11 | async-start | bytes 1179648
  317.2 145.3 %collective-permute-start.27 = (f32[2,40,512]{2,1,0:T(8,128)}, f32[2,40,512]{2,1,0:T(8,128)}, u32[]{:S(2)}, u32[]{:S(2)}) collective-permute-start(f32[2,40,512]{2,1,0:T(8,128)} %get-tuple-element.68), channel_id=1, source_target_pairs={{0,8},{8,16},{16,24},{1,9},{9,17},{17,25},{2,10},{10,18},{18,26},{... | collective-permute-start | bytes 491528 | tf_op jit(solution)/shard_map/ppermute | solution.py:17
  322.4 141.9 %collective-permute-start.26 = (f32[2,40,512]{2,1,0:T(8,128)}, f32[2,40,512]{2,1,0:T(8,128)}, u32[]{:S(2)}, u32[]{:S(2)}) collective-permute-start(f32[2,40,512]{2,1,0:T(8,128)} %get-tuple-element.67), channel_id=1, source_target_pairs={{8,0},{16,8},{24,16},{9,1},{17,9},{25,17},{10,2},{18,10},{26,18},{... | collective-permute-start | bytes 491528 | tf_op jit(solution)/shard_map/ppermute | solution.py:17
  323.7 143.1 %collective-permute-start.24 = (f32[2,160,1]{2,1,0:T(8,128)}, f32[2,160,1]{2,1,0:T(8,128)}, u32[]{:S(2)}, u32[]{:S(2)}) collective-permute-start(f32[2,160,1]{2,1,0:T(8,128)} %get-tuple-element.63), channel_id=1, source_target_pairs={{0,1},{1,2},{2,3},{3,4},{4,5},{5,6},{6,7},{8,9},{9,10},{10,11},{11... | collective-permute-start | bytes 3848 | tf_op jit(solution)/shard_map/ppermute | solution.py:33
  326.3 140.5 %collective-permute-start.25 = (f32[2,160,1]{2,1,0:T(8,128)}, f32[2,160,1]{2,1,0:T(8,128)}, u32[]{:S(2)}, u32[]{:S(2)}) collective-permute-start(f32[2,160,1]{2,1,0:T(8,128)} %get-tuple-element.64), channel_id=1, source_target_pairs={{1,0},{2,1},{3,2},{4,3},{5,4},{6,5},{7,6},{9,8},{10,9},{11,10},{12... | collective-permute-start | bytes 3848 | tf_op jit(solution)/shard_map/ppermute | solution.py:35
  348.3 16.6 %collective-permute-start.17 = (f32[2,256]{1,0:T(2,128)S(1)}, f32[2,256]{1,0:T(2,128)S(1)}, u32[]{:S(2)}, u32[]{:S(2)}) collective-permute-start(f32[2,256]{1,0:T(2,128)S(1)} %get-tuple-element.115), channel_id=1, source_target_pairs={{0,8},{8,16},{16,24},{1,9},{9,17},{17,25},{2,10},{10,18},{18,26},{... | collective-permute-start | bytes 6152 | tf_op jit(solution)/shard_map/ppermute | solution.py:17
  364.9 16.1 %collective-permute-start.16 = (f32[2,256]{1,0:T(2,128)S(1)}, f32[2,256]{1,0:T(2,128)S(1)}, u32[]{:S(2)}, u32[]{:S(2)}) collective-permute-start(f32[2,256]{1,0:T(2,128)S(1)} %get-tuple-element.114), channel_id=1, source_target_pairs={{8,0},{16,8},{24,16},{9,1},{17,9},{25,17},{10,2},{18,10},{26,18},{... | collective-permute-start | bytes 6152 | tf_op jit(solution)/shard_map/ppermute | solution.py:17
  380.9 118.7 %reduce-scatter.33.cloned.1.call-start = ((), (), s32[]{:S(2)}) async-start(), calls=%async_computation.12 | async-start | bytes 1179648
  453.4 131.8 %reduce-scatter.35.cloned.1.call-start = ((), (), s32[]{:S(2)}) async-start(), calls=%async_computation.13 | async-start | bytes 1179648
  489.5 58.4 %collective-permute-start.33 = (f32[2,40,512]{2,1,0:T(8,128)}, f32[2,40,512]{2,1,0:T(8,128)}, u32[]{:S(2)}, u32[]{:S(2)}) collective-permute-start(f32[2,40,512]{2,1,0:T(8,128)} %get-tuple-element.59), channel_id=1, source_target_pairs={{0,8},{8,16},{16,24},{1,9},{9,17},{17,25},{2,10},{10,18},{18,26},{... | collective-permute-start | bytes 491528 | tf_op jit(solution)/shard_map/ppermute | solution.py:17
  494.7 55.1 %collective-permute-start.32 = (f32[2,40,512]{2,1,0:T(8,128)}, f32[2,40,512]{2,1,0:T(8,128)}, u32[]{:S(2)}, u32[]{:S(2)}) collective-permute-start(f32[2,40,512]{2,1,0:T(8,128)} %get-tuple-element.58), channel_id=1, source_target_pairs={{8,0},{16,8},{24,16},{9,1},{17,9},{25,17},{10,2},{18,10},{26,18},{... | collective-permute-start | bytes 491528 | tf_op jit(solution)/shard_map/ppermute | solution.py:17
  495.9 56.3 %collective-permute-start.30 = (f32[2,160,1]{2,1,0:T(8,128)}, f32[2,160,1]{2,1,0:T(8,128)}, u32[]{:S(2)}, u32[]{:S(2)}) collective-permute-start(f32[2,160,1]{2,1,0:T(8,128)} %get-tuple-element.54), channel_id=1, source_target_pairs={{0,1},{1,2},{2,3},{3,4},{4,5},{5,6},{6,7},{8,9},{9,10},{10,11},{11... | collective-permute-start | bytes 3848 | tf_op jit(solution)/shard_map/ppermute | solution.py:33
  497.9 54.3 %collective-permute-start.31 = (f32[2,160,1]{2,1,0:T(8,128)}, f32[2,160,1]{2,1,0:T(8,128)}, u32[]{:S(2)}, u32[]{:S(2)}) collective-permute-start(f32[2,160,1]{2,1,0:T(8,128)} %get-tuple-element.55), channel_id=1, source_target_pairs={{1,0},{2,1},{3,2},{4,3},{5,4},{6,5},{7,6},{9,8},{10,9},{11,10},{12... | collective-permute-start | bytes 3848 | tf_op jit(solution)/shard_map/ppermute | solution.py:35
  519.7 15.9 %collective-permute-start.28 = (f32[2,256]{1,0:T(2,128)}, f32[2,256]{1,0:T(2,128)}, u32[]{:S(2)}, u32[]{:S(2)}) collective-permute-start(f32[2,256]{1,0:T(2,128)} %get-tuple-element.106), channel_id=1, source_target_pairs={{8,0},{16,8},{24,16},{9,1},{17,9},{25,17},{10,2},{18,10},{26,18},{... | collective-permute-start | bytes 6152 | tf_op jit(solution)/shard_map/ppermute | solution.py:17
  535.6 126.1 %reduce-scatter.37.cloned.1.call-start = ((), (), s32[]{:S(2)}) async-start(), calls=%async_computation.14 | async-start | bytes 1179648
  575.2 90.3 %collective-permute-start.39 = (f32[2,40,512]{2,1,0:T(8,128)}, f32[2,40,512]{2,1,0:T(8,128)}, u32[]{:S(2)}, u32[]{:S(2)}) collective-permute-start(f32[2,40,512]{2,1,0:T(8,128)} %get-tuple-element.50), channel_id=1, source_target_pairs={{0,8},{8,16},{16,24},{1,9},{9,17},{17,25},{2,10},{10,18},{18,26},{... | collective-permute-start | bytes 491528 | tf_op jit(solution)/shard_map/ppermute | solution.py:17
  580.6 86.7 %collective-permute-start.38 = (f32[2,40,512]{2,1,0:T(8,128)}, f32[2,40,512]{2,1,0:T(8,128)}, u32[]{:S(2)}, u32[]{:S(2)}) collective-permute-start(f32[2,40,512]{2,1,0:T(8,128)} %get-tuple-element.49), channel_id=1, source_target_pairs={{8,0},{16,8},{24,16},{9,1},{17,9},{25,17},{10,2},{18,10},{26,18},{... | collective-permute-start | bytes 491528 | tf_op jit(solution)/shard_map/ppermute | solution.py:17
  581.9 87.9 %collective-permute-start.36 = (f32[2,160,1]{2,1,0:T(8,128)}, f32[2,160,1]{2,1,0:T(8,128)}, u32[]{:S(2)}, u32[]{:S(2)}) collective-permute-start(f32[2,160,1]{2,1,0:T(8,128)} %get-tuple-element.45), channel_id=1, source_target_pairs={{0,1},{1,2},{2,3},{3,4},{4,5},{5,6},{6,7},{8,9},{9,10},{10,11},{11... | collective-permute-start | bytes 3848 | tf_op jit(solution)/shard_map/ppermute | solution.py:33
  583.9 85.9 %collective-permute-start.37 = (f32[2,160,1]{2,1,0:T(8,128)}, f32[2,160,1]{2,1,0:T(8,128)}, u32[]{:S(2)}, u32[]{:S(2)}) collective-permute-start(f32[2,160,1]{2,1,0:T(8,128)} %get-tuple-element.46), channel_id=1, source_target_pairs={{1,0},{2,1},{3,2},{4,3},{5,4},{6,5},{7,6},{9,8},{10,9},{11,10},{12... | collective-permute-start | bytes 3848 | tf_op jit(solution)/shard_map/ppermute | solution.py:35
  605.3 15.9 %collective-permute-start.34 = (f32[2,256]{1,0:T(2,128)}, f32[2,256]{1,0:T(2,128)}, u32[]{:S(2)}, u32[]{:S(2)}) collective-permute-start(f32[2,256]{1,0:T(2,128)} %get-tuple-element.102), channel_id=1, source_target_pairs={{8,0},{16,8},{24,16},{9,1},{17,9},{25,17},{10,2},{18,10},{26,18},{... | collective-permute-start | bytes 6152 | tf_op jit(solution)/shard_map/ppermute | solution.py:17
  621.2 152.9 %reduce-scatter.39.cloned.1.call-start = ((), (), s32[]{:S(2)}) async-start(), calls=%async_computation.15 | async-start | bytes 1179648
  707.6 67.8 %collective-permute-start.45 = (f32[2,40,512]{2,1,0:T(8,128)}, f32[2,40,512]{2,1,0:T(8,128)}, u32[]{:S(2)}, u32[]{:S(2)}) collective-permute-start(f32[2,40,512]{2,1,0:T(8,128)} %get-tuple-element.41), channel_id=1, source_target_pairs={{0,8},{8,16},{16,24},{1,9},{9,17},{17,25},{2,10},{10,18},{18,26},{... | collective-permute-start | bytes 491528 | tf_op jit(solution)/shard_map/ppermute | solution.py:17
  711.7 65.6 %collective-permute-start.44 = (f32[2,40,512]{2,1,0:T(8,128)}, f32[2,40,512]{2,1,0:T(8,128)}, u32[]{:S(2)}, u32[]{:S(2)}) collective-permute-start(f32[2,40,512]{2,1,0:T(8,128)} %get-tuple-element.40), channel_id=1, source_target_pairs={{8,0},{16,8},{24,16},{9,1},{17,9},{25,17},{10,2},{18,10},{26,18},{... | collective-permute-start | bytes 491528 | tf_op jit(solution)/shard_map/ppermute | solution.py:17
  712.9 66.8 %collective-permute-start.42 = (f32[2,160,1]{2,1,0:T(8,128)}, f32[2,160,1]{2,1,0:T(8,128)}, u32[]{:S(2)}, u32[]{:S(2)}) collective-permute-start(f32[2,160,1]{2,1,0:T(8,128)} %get-tuple-element.36), channel_id=1, source_target_pairs={{0,1},{1,2},{2,3},{3,4},{4,5},{5,6},{6,7},{8,9},{9,10},{10,11},{11... | collective-permute-start | bytes 3848 | tf_op jit(solution)/shard_map/ppermute | solution.py:33
  714.9 64.8 %collective-permute-start.43 = (f32[2,160,1]{2,1,0:T(8,128)}, f32[2,160,1]{2,1,0:T(8,128)}, u32[]{:S(2)}, u32[]{:S(2)}) collective-permute-start(f32[2,160,1]{2,1,0:T(8,128)} %get-tuple-element.37), channel_id=1, source_target_pairs={{1,0},{2,1},{3,2},{4,3},{5,4},{6,5},{7,6},{9,8},{10,9},{11,10},{12... | collective-permute-start | bytes 3848 | tf_op jit(solution)/shard_map/ppermute | solution.py:35
  716.3 16.2 %collective-permute-start.40 = (f32[2,256]{1,0:T(2,128)}, f32[2,256]{1,0:T(2,128)}, u32[]{:S(2)}, u32[]{:S(2)}) collective-permute-start(f32[2,256]{1,0:T(2,128)} %get-tuple-element.98), channel_id=1, source_target_pairs={{8,0},{16,8},{24,16},{9,1},{17,9},{25,17},{10,2},{18,10},{26,18},{... | collective-permute-start | bytes 6152 | tf_op jit(solution)/shard_map/ppermute | solution.py:17
  783.4 36.2 %collective-permute-start.49 = (f32[2,40,512]{2,1,0:T(8,128)}, f32[2,40,512]{2,1,0:T(8,128)}, u32[]{:S(2)}, u32[]{:S(2)}) collective-permute-start(f32[2,40,512]{2,1,0:T(8,128)} %get-tuple-element.29), channel_id=1, source_target_pairs={{0,8},{8,16},{16,24},{1,9},{9,17},{17,25},{2,10},{10,18},{18,26},{... | collective-permute-start | bytes 491528 | tf_op jit(solution)/shard_map/ppermute | solution.py:17
  787.4 33.7 %collective-permute-start.48 = (f32[2,40,512]{2,1,0:T(8,128)}, f32[2,40,512]{2,1,0:T(8,128)}, u32[]{:S(2)}, u32[]{:S(2)}) collective-permute-start(f32[2,40,512]{2,1,0:T(8,128)} %get-tuple-element.28), channel_id=1, source_target_pairs={{8,0},{16,8},{24,16},{9,1},{17,9},{25,17},{10,2},{18,10},{26,18},{... | collective-permute-start | bytes 491528 | tf_op jit(solution)/shard_map/ppermute | solution.py:17
  789.6 33.8 %collective-permute-start.46 = (f32[2,160,1]{2,1,0:T(8,128)}, f32[2,160,1]{2,1,0:T(8,128)}, u32[]{:S(2)}, u32[]{:S(2)}) collective-permute-start(f32[2,160,1]{2,1,0:T(8,128)} %get-tuple-element.30), channel_id=1, source_target_pairs={{0,1},{1,2},{2,3},{3,4},{4,5},{5,6},{6,7},{8,9},{9,10},{10,11},{11... | collective-permute-start | bytes 3848 | tf_op jit(solution)/shard_map/ppermute | solution.py:33
  791.6 31.9 %collective-permute-start.47 = (f32[2,160,1]{2,1,0:T(8,128)}, f32[2,160,1]{2,1,0:T(8,128)}, u32[]{:S(2)}, u32[]{:S(2)}) collective-permute-start(f32[2,160,1]{2,1,0:T(8,128)} %get-tuple-element.32), channel_id=1, source_target_pairs={{1,0},{2,1},{3,2},{4,3},{5,4},{6,5},{7,6},{9,8},{10,9},{11,10},{12... | collective-permute-start | bytes 3848 | tf_op jit(solution)/shard_map/ppermute | solution.py:35
  (84 other events, 1752.7 us)
Sparse Core Ops, SparseCore 0:
  112.0 37.5 reduce-scatter.24
  210.9 40.3 reduce-scatter.26
  297.2 37.7 reduce-scatter.28
  381.1 37.1 reduce-scatter.30
  453.5 38.0 reduce-scatter.32
  535.7 40.8 reduce-scatter.34
  621.3 40.4 reduce-scatter.36
  732.6 41.4 reduce-scatter.38
where the time goes:
time: 847 us; the launch traced here: 834 us
  blocking collectives  191 us (23%)
  matrix products  174 us (21%)
  waiting for transfers between devices  157 us (19%)
  local copies, waits for them, and re-layouts  136 us (16%)
  starting transfers between devices  129 us (15%)
  other arithmetic  31.5 us (4%)
  between operations  16.9 us (2%)
    unnamed x16, waiting for transfers between devices  155 us
    ppermute x34, starting transfers between devices, from_behind(): return lax.ppermute(block, axis, route)  97.6 us
    unnamed x181, local copies, waits for them, and re-layouts  95.9 us
    psum x7, blocking collectives, reduce_partials(): boundary = lax.psum(partial_boundary, 'outer')  93.1 us
    all_gather x8, blocking collectives, local(): gathered = lax.all_gather(extended, 'outer', axis=2, tiled=True)  82.9 us
    dot_general x8, matrix products, local(): jnp.einsum('lij,plj->pli', dipole, gathered[:, 1:], precision=highest)  79.2 us
    dot_general x8, matrix products, local(): jnp.einsum('lji,plj->pli', source_blocks, source_rows, precision=highest)  55.2 us
    ppermute x8, starting transfers between devices, with_halo(): lax.ppermute(tail, axis, [(i, (i + 1) % count) for i in range(ends)])  20 us
  transfers between devices with their start and end apart: 58, of which 9 were waited for; matrix products, arithmetic and copies ran while one was open for 36% of the time, Pallas kernels for 0%

commit v1 on v0

v1 whole, which is shorter than its diff:
```python
import functools

import jax
import jax.numpy as jnp
from jax import lax
from jax.experimental import pallas as pl
from jax.experimental.pallas import tpu as pltpu
from jax.sharding import PartitionSpec as P

STEPS = 2
ORDER = 4

kinetic_scale = 3.125
time_step = 0.1

MESH = pl.DeviceIdType.MESH
f32 = jnp.float32
bf16 = jnp.bfloat16
NT = (((1,), (1,)), ((), ()))
NN = (((1,), (0,)), ((), ()))


def split(x):
    high = x.astype(bf16)
    return high, (x - high.astype(f32)).astype(bf16)


def kernel(
    planes,
    sectors,
    ch,
    inner_ref,
    outer_ref,
    live_ref,
    energy_ref,
    dipole_ref,
    surface_ref,
    diag_ref,
    mix_ref,
    field_ref,
    inner_out,
    outer_out,
    dip_hi,
    dip_lo,
    mix_split,
    grid,
    term,
    peer_in,
    above_in,
    part_out,
    part_in,
    below_in,
    mixed,
    sem_a_send,
    sem_a_recv,
    sem_z_send,
    sem_z_recv,
    sem_b_send,
    sem_b_recv,
    sem_y_send,
    sem_y_recv,
    sem_up_send,
    sem_up_recv,
    sem_down_send,
    sem_down_recv,
):
    z = lax.axis_index("inner")
    me = lax.axis_index("outer")
    rows, rc = inner_ref.shape
    blocks = rows // 2
    nc, nr = outer_ref.shape[1:]
    total = rc * sectors
    width = peer_in.shape[3]
    has_below = z > 0
    has_above = z < planes - 1

    @pl.when(z == 0)
    def _():
        below_in[...] = jnp.zeros_like(below_in)
        grid[:, :, 0:ch, :] = jnp.zeros((2, 2, ch, nr), f32)

    @pl.when(z == planes - 1)
    def _():
        above_in[...] = jnp.zeros_like(above_in)
        grid[:, :, ch + nc : 2 * ch + nc, :] = jnp.zeros((2, 2, ch, nr), f32)

    term[...] = inner_ref[...] * live_ref[...]
    inner_out[...] = term[...]
    for p in range(2):
        x = outer_ref[p]
        grid[0, p, ch : ch + nc, :] = x
        outer_out[p] = x
    mh, ml = split(mix_ref[...])
    mix_split[0:nc, :] = mh
    mix_split[nc : 2 * nc, :] = ml

    def split_rows(i, carry):
        at = pl.ds(pl.multiple_of(i * 16, 16), 16)
        high, low = split(dipole_ref[at, :])
        dip_hi[at, :] = high
        dip_lo[at, :] = low
        return carry

    lax.fori_loop(0, blocks * rc // 16, split_rows, 0)

    eye = lax.broadcasted_iota(jnp.int32, (nc, width), 0) == lax.broadcasted_iota(
        jnp.int32, (nc, width), 1
    )

    def to_row(col):
        return jnp.sum(jnp.where(eye, col, 0.0), axis=0, keepdims=True)

    def to_col(row):
        return jnp.sum(jnp.where(eye, row, 0.0), axis=1, keepdims=True)

    def wait(ref, sem):
        pltpu.make_async_copy(ref, ref, sem).wait()

    def apply(t, carry):
        par = lax.rem(t, 2)
        nxt = 1 - par
        order = lax.rem(t, ORDER)
        strength = field_ref[lax.div(t, ORDER)]
        factor = time_step / (order + 1).astype(f32)
        last = order == ORDER - 1

        up = pltpu.make_async_remote_copy(
            src_ref=grid.at[par, :, pl.ds(nc, ch), :],
            dst_ref=grid.at[par, :, pl.ds(0, ch), :],
            send_sem=sem_up_send,
            recv_sem=sem_up_recv.at[par],
            device_id={"inner": z + 1, "outer": me},
            device_id_type=MESH,
        )
        down = pltpu.make_async_remote_copy(
            src_ref=grid.at[par, :, pl.ds(ch, ch), :],
            dst_ref=grid.at[par, :, pl.ds(ch + nc, ch), :],
            send_sem=sem_down_send,
            recv_sem=sem_down_recv.at[par],
            device_id={"inner": z - 1, "outer": me},
            device_id_type=MESH,
        )

        c = term[...]
        peer_in[par, me, 0:rows, 0:rc] = c
        edge_rows = []
        for p in range(2):
            edge_rows.append(to_row(grid[par, p, ch : ch + nc, 0:1]))
        for p in range(2):
            edge_rows.append(to_row(grid[par, p, ch : ch + nc, nr - 1 : nr]))
        for p in range(2):
            spread = jnp.concatenate(
                [
                    jnp.broadcast_to(c[2 * l + p : 2 * l + p + 1], (ch, rc))
                    for l in range(blocks)
                ],
                axis=0,
            )
            edge_rows.append(
                to_row(jnp.sum(surface_ref[...] * spread, axis=1, keepdims=True))
            )
        edge_rows.append(jnp.zeros((2, width), f32))
        peer_in[par, me, rows : rows + 8, :] = jnp.concatenate(edge_rows, axis=0)

        def send_a(s, k):
            to = lax.rem(me + s, sectors)
            pltpu.make_async_remote_copy(
                src_ref=peer_in.at[par, me],
                dst_ref=peer_in.at[par, me],
                send_sem=sem_a_send,
                recv_sem=sem_a_recv.at[par],
                device_id={"inner": z, "outer": to},
                device_id_type=MESH,
            ).start()
            return k

        lax.fori_loop(1, sectors, send_a, 0)

        @pl.when(has_below)
        def _():
            def send_z(s, k):
                to = lax.rem(me + s, sectors)
                pltpu.make_async_remote_copy(
                    src_ref=peer_in.at[par, me, pl.ds(0, rows), pl.ds(0, rc)],
                    dst_ref=above_in.at[par, me],
                    send_sem=sem_z_send,
                    recv_sem=sem_z_recv.at[par],
                    device_id={"inner": z - 1, "outer": to},
                    device_id_type=MESH,
                ).start()
                return k

            lax.fori_loop(0, sectors, send_z, 0)
            down.start()

        row_block = lax.broadcasted_iota(jnp.int32, (rows, 1), 0) // 2
        ch_, cl_ = split(c)
        both = jnp.concatenate([ch_, cl_], axis=0)
        back = jnp.zeros((rows, total), f32)
        for l in range(blocks):
            at = pl.ds(l * rc, rc)
            r = lax.dot_general(both, dip_hi[at, :], NN, preferred_element_type=f32)
            q = lax.dot_general(ch_, dip_lo[at, :], NN, preferred_element_type=f32)
            back = jnp.where(row_block == l, r[:rows] + r[rows:] + q, back)
        back = pltpu.roll(back, 2, 0)
        for k in range(sectors):
            part_out[k] = back[:, k * rc : (k + 1) * rc]
        part_in[par, me] = part_out[me]

        @pl.when(has_above)
        def _():
            def send_y(s, k):
                to = lax.rem(me + s, sectors)
                pltpu.make_async_remote_copy(
                    src_ref=part_out.at[to],
                    dst_ref=below_in.at[par, me],
                    send_sem=sem_y_send,
                    recv_sem=sem_y_recv.at[par],
                    device_id={"inner": z + 1, "outer": to},
                    device_id_type=MESH,
                ).start()
                return k

            lax.fori_loop(0, sectors, send_y, 0)
            up.start()

        def send_b(s, k):
            to = lax.rem(me + s, sectors)
            pltpu.make_async_remote_copy(
                src_ref=part_out.at[to],
                dst_ref=part_in.at[par, me],
                send_sem=sem_b_send,
                recv_sem=sem_b_recv.at[par],
                device_id={"inner": z, "outer": to},
                device_id_type=MESH,
            ).start()
            return k

        lax.fori_loop(1, sectors, send_b, 0)

        wait(peer_in.at[par, pl.ds(0, sectors - 1)], sem_a_recv.at[par])

        @pl.when(has_above)
        def _():
            wait(above_in.at[par], sem_z_recv.at[par])

        def forward_rows(values, l):
            vh, vl = values
            at = pl.ds(l * rc, rc)
            r = lax.dot_general(
                jnp.concatenate([vh, vl], axis=0), dip_hi[at, :], NT, preferred_element_type=f32
            )
            q = lax.dot_general(vh, dip_lo[at, :], NT, preferred_element_type=f32)
            return r[:rows] + r[rows:] + q

        own = split(
            jnp.concatenate([peer_in[par, k, 0:rows, 0:rc] for k in range(sectors)], axis=1)
        )
        other = split(jnp.concatenate([above_in[par, k] for k in range(sectors)], axis=1))
        ahead = jnp.zeros((rows, rc), f32)
        for l in range(blocks):
            if l < blocks - 1:
                ahead = jnp.where(row_block == l + 1, forward_rows(own, l), ahead)
            else:
                ahead = jnp.where(row_block == 0, forward_rows(other, l), ahead)
        ahead = pltpu.roll(ahead, rows - 2, 0)

        surf = []
        edge = peer_in[par, 0, rows : rows + 8, :]
        for p in range(2):
            prod = surface_ref[...] * to_col(edge[p : p + 1])
            surf.append(
                [
                    jnp.sum(prod[l * ch : (l + 1) * ch], axis=0, keepdims=True)
                    for l in range(blocks)
                ]
            )
        surf = jnp.concatenate(
            [surf[p][l] for l in range(blocks) for p in range(2)], axis=0
        )

        @pl.when(has_below)
        def _():
            wait(grid.at[par, :, pl.ds(0, ch), :], sem_up_recv.at[par])

        @pl.when(has_above)
        def _():
            wait(grid.at[par, :, pl.ds(0, ch), :], sem_down_recv.at[par])

        bound = jnp.zeros((8, width), f32)
        for k in range(sectors):
            bound = bound + peer_in[par, k, rows : rows + 8, :]
        before = peer_in[par, lax.rem(me + sectors - 1, sectors), rows : rows + 8, :]
        after = peer_in[par, lax.rem(me + 1, sectors), rows : rows + 8, :]
        lane = lax.broadcasted_iota(jnp.int32, (1, nr), 1)
        for p in range(2):
            gh, gl = split(grid[par, p])
            r = lax.dot_general(mix_split[...], gh, NN, preferred_element_type=f32)
            q = lax.dot_general(mix_split[0:nc, :], gl, NN, preferred_element_type=f32)
            coupled = r[:nc] + r[nc:] + q
            left_row = jnp.where(me == 0, bound[4 + p : 5 + p], before[2 + p : 3 + p])
            right_row = jnp.where(me == sectors - 1, 0.0, after[p : p + 1])
            left_col = to_col(left_row)
            right_col = to_col(right_row)
            x = grid[par, p, ch : ch + nc, :]
            left = jnp.where(lane == 0, left_col, pltpu.roll(x, 1, 1))
            right = jnp.where(lane == nr - 1, right_col, pltpu.roll(x, nr - 1, 1))
            image = diag_ref[...] * x - kinetic_scale * (left + right) + strength * coupled
            value = (factor if p == 1 else -factor) * image
            acc = outer_out[1 - p] + value
            outer_out[1 - p] = acc
            grid[nxt, 1 - p, ch : ch + nc, :] = jnp.where(last, acc, value)

        wait(part_in.at[par, pl.ds(0, sectors - 1)], sem_b_recv.at[par])

        @pl.when(has_below)
        def _():
            wait(below_in.at[par], sem_y_recv.at[par])

        near = part_in[par, 0]
        far = below_in[par, 0]
        for k in range(1, sectors):
            near = near + part_in[par, k]
            far = far + below_in[par, k]
        behind = jnp.where(row_block == 0, far, near)
        image = live_ref[...] * (
            energy_ref[...] * c + strength * (ahead + behind) - kinetic_scale * surf
        )
        even = lax.rem(lax.broadcasted_iota(jnp.int32, (rows, 1), 0), 2) == 0
        value = factor * jnp.where(
            even, pltpu.roll(image, rows - 1, 0), -pltpu.roll(image, 1, 0)
        )
        acc = inner_out[...] + value
        inner_out[...] = acc
        term[...] = jnp.where(last, acc, value)

        wait(peer_in.at[par, pl.ds(0, sectors - 1)], sem_a_send)
        wait(part_in.at[par, pl.ds(0, sectors - 1)], sem_b_send)

        @pl.when(has_below)
        def _():
            wait(above_in.at[par], sem_z_send)
            down.wait_send()

        @pl.when(has_above)
        def _():
            wait(below_in.at[par], sem_y_send)
            up.wait_send()

        return carry

    lax.fori_loop(0, STEPS * ORDER, apply, 0)


def local(
    planes,
    sectors,
    inner_state,
    outer_state,
    energies,
    dipole,
    surface,
    thresholds,
    coupling_coef,
    coupling_pattern,
    block_sizes,
    field_strength,
):
    blocks, rc, total = dipole.shape
    ch = coupling_coef.shape[1]
    nc, nr = outer_state.shape[1:]
    rows = 2 * blocks
    width = max(rc, -(-nc // 128) * 128)
    row_index = lax.axis_index("outer") * rc + jnp.arange(rc, dtype=jnp.int32)
    live = (row_index[None, :] < block_sizes[:, None]).astype(f32)
    coupling = coupling_coef * coupling_pattern.astype(f32)
    below = lax.ppermute(coupling[blocks - 1], "inner", [(i, i + 1) for i in range(planes - 1)])
    mix = jnp.zeros((nc, nc + 2 * ch), f32)
    for l in range(blocks):
        source = below if l == 0 else coupling[l - 1]
        mix = mix.at[l * ch : (l + 1) * ch, l * ch : (l + 1) * ch].set(source.T)
        mix = mix.at[l * ch : (l + 1) * ch, (l + 2) * ch : (l + 3) * ch].set(coupling[l])
    diag = (thresholds + 2.0 * kinetic_scale)[:, None]
    vmem = pl.BlockSpec(memory_space=pltpu.VMEM)
    dma = pltpu.SemaphoreType.DMA
    inner_final, outer_final = pl.pallas_call(
        functools.partial(kernel, planes, sectors, ch),
        out_shape=(
            jax.ShapeDtypeStruct((rows, rc), f32),
            jax.ShapeDtypeStruct((2, nc, nr), f32),
        ),
        in_specs=[vmem] * 8 + [pl.BlockSpec(memory_space=pltpu.SMEM)],
        out_specs=(vmem, vmem),
        scratch_shapes=[
            pltpu.VMEM((blocks * rc, total), bf16),
            pltpu.VMEM((blocks * rc, total), bf16),
            pltpu.VMEM((2 * nc, nc + 2 * ch), bf16),
            pltpu.VMEM((2, 2, nc + 2 * ch, nr), f32),
            pltpu.VMEM((rows, rc), f32),
            pltpu.VMEM((2, sectors, rows + 8, width), f32),
            pltpu.VMEM((2, sectors, rows, rc), f32),
            pltpu.VMEM((sectors, rows, rc), f32),
            pltpu.VMEM((2, sectors, rows, rc), f32),
            pltpu.VMEM((2, sectors, rows, rc), f32),
            pltpu.VMEM((8, 128), f32),
            dma(()), dma((2,)), dma(()), dma((2,)),
            dma(()), dma((2,)), dma(()), dma((2,)),
            dma(()), dma((2,)), dma(()), dma((2,)),
        ],
        compiler_params=pltpu.CompilerParams(
            has_side_effects=True, vmem_limit_bytes=56 * 1024 * 1024
        ),
    )(
        inner_state.transpose(1, 0, 2).reshape(rows, rc),
        outer_state,
        jnp.repeat(live, 2, axis=0),
        jnp.repeat(energies, 2, axis=0),
        dipole.reshape(blocks * rc, total),
        surface.reshape(nc, rc),
        diag,
        mix,
        field_strength,
    )
    return inner_final.reshape(blocks, 2, rc).transpose(1, 0, 2), outer_final


def solution(mesh):
    placed = (
        P(None, "inner", "outer"),
        P(None, "inner", "outer"),
        P("inner", "outer"),
        P("inner", "outer", None),
        P("inner", None, "outer"),
        P("inner"),
        P("inner", None, None),
        P("inner", None, None),
        P("inner"),
        P(),
    )
    return jax.shard_map(
        functools.partial(local, mesh.shape["inner"], mesh.shape["outer"]),
        mesh=mesh,
        in_specs=placed,
        out_specs=(P(None, "inner", "outer"), P(None, "inner", "outer")),
        check_vma=False,
    )
```

time: 847 us -> 113 us (0.13); the launches traced: 834 us -> 113 us
  blocking collectives: 191 us -> 0 us
  matrix products: 174 us -> 0 us
  waiting for transfers between devices: 157 us -> 0.01 us
  starting transfers between devices: 129 us -> 4.96 us
  local copies, waits for them, and re-layouts: 136 us -> 19.9 us
  Pallas kernels: 0 us -> 82.7 us
  other arithmetic: 31.5 us -> 4.3 us
  between operations: 16.9 us -> 0.77 us
    dot_general x48 -> x0, matrix products: 174 us -> none  [the longest x8 79.2 us: local(): jnp.einsum('lij,plj->pli', dipole, gathered[:, 1:], precision=highest)]
    unnamed x16 -> x0, waiting for transfers between devices: 155 us -> none
    ppermute x50 -> x1, starting transfers between devices: 128 us -> 4.96 us  [local(): lax.ppermute(coupling[blocks - 1], 'inner', [(i, i + 1) for i in range(pl...]
    psum x8 -> x0, blocking collectives: 108 us -> none  [the longest x7 93.1 us: reduce_partials(): boundary = lax.psum(partial_boundary, 'outer')]
    unnamed x181 -> x4, local copies, waits for them, and re-layouts: 95.9 us -> 2.7 us
    all_gather x8 -> x0, blocking collectives: 82.9 us -> none  [local(): gathered = lax.all_gather(extended, 'outer', axis=2, tiled=True)]
    pallas_call x0 -> x1, Pallas kernels: none -> 82.7 us  [local(): pl.pallas_call(functools.partial(kernel, planes, sectors, ch), out_shape=...]
    slice x20 -> x0, local copies, waits for them, and re-layouts: 17.3 us -> none  [the longest x8 9.79 us: local(): channel_grid[:, 1:]]
  transfers between devices with their start and end apart: 58 -> 1, of which waited for: 9 -> 0; matrix products, arithmetic and copies ran while one was open for 36% -> 7% of each run, Pallas kernels for 0% -> 0%
where the time goes in v1:
time: 113 us
  Pallas kernels  82.7 us (73%)
  local copies, waits for them, and re-layouts  19.9 us (18%)
  starting transfers between devices  4.96 us (4%)
  other arithmetic  4.3 us (4%)
    pallas_call x1, Pallas kernels, local(): pl.pallas_call(functools.partial(kernel, planes, sectors, ch), out_shape=...  82.7 us
    scatter x4, local copies, waits for them, and re-layouts, local(): mix.at[l * ch:(l + 1) * ch, (l + 2) * ch:(l + 3) * ch].set(coupling[l])  5.73 us
    ppermute x1, starting transfers between devices, local(): lax.ppermute(coupling[blocks - 1], 'inner', [(i, i + 1) for i in range(pl...  4.96 us
    scatter x5, local copies, waits for them, and re-layouts, local(): mix = mix.at[l * ch:(l + 1) * ch, l * ch:(l + 1) * ch].set(source.T)  3.97 us
    unnamed x4, local copies, waits for them, and re-layouts  2.7 us
  transfers between devices with their start and end apart: 1, of which 0 were waited for; matrix products, arithmetic and copies ran while one was open for 7% of the time, Pallas kernels for 0%

profile of v1, /device:TPU:0, one launch (start us, length us, event | category | flops | bytes accessed | tf_op | source)
XLA Modules:
  0.0 112.5 jit_solution(3531209117891132489)
XLA Ops:
  0.6 0.9 convert_multiply_fusion
  1.6 5.0 %collective-permute-start = (f32[40,40]{1,0:T(8,128)S(1)}, f32[40,40]{1,0:T(8,128)S(1)}, u32[]{:S(2)}, u32[]{:S(2)}) collective-permute-start(f32[40,40]{1,0:T(8,128)S(1)} %get-tuple-element.107), channel_id=1, source_target_pairs={{0,8},{8,16},{16,24},{1,9},{9,17},{17,25},{2,10},{10,18},{18,26},{... | collective-permute-start | bytes 19208 | tf_op jit(solution)/shard_map/ppermute | solution.py:377
  6.6 1.3 %and_reduce_fusion = pred[]{:T(512)} fusion(s32[2]{0:T(128)} %constant.212.clone.1), kind=kLoop, calls=%fused_computation.11 | loop fusion | flops 9 | bytes 9 | tf_op jit(solution)/shard_map/reduce.9
  7.9 0.7 broadcast_add_fusion
  8.6 0.7 compare_convert_fusion
  9.3 0.6 fusion
  9.9 0.6 reshape.273.live_ref
  10.5 0.7 copy.19
  11.2 0.6 reshape.272.inner_ref
  11.8 0.7 broadcast_in_dim.13
  12.5 0.6 reshape.274.energy_ref
  13.1 0.7 copy.25.diag_ref
  13.8 0.1 copy.23
  13.9 0.1 copy.22
  14.0 0.0 collective-permute-done
  14.0 1.4 %pad_dynamic-slice_fusion = f32[40,40]{0,1:T(8,128)S(1)} fusion(s32[]{:T(128)} %bitcast.7, s32[]{:T(128)} %bitcast.8, f32[40,40]{0,1:T(8,128)S(1)} %bitcast.29), kind=kLoop, calls=%fused_computation | loop fusion | bytes 12808 | tf_op jit(solution)/shard_map/dynamic-slice.29
  15.4 0.1 copy.27
  15.4 0.6 bitcast_select_fusion
  16.1 0.1 copy.21
  16.2 2.3 %scatter.29 = f32[160,240]{0,1:T(8,128)S(1)} dynamic-update-slice(f32[160,240]{0,1:T(8,128)S(1)} %scatter.26, f32[40,40]{0,1:T(8,128)S(1)} %copy.21, s32[]{:T(128)} %bitcast.7, s32[]{:T(128)} %bitcast.8) | dynamic-update-slice | bytes 12804 | tf_op jit(solution)/shard_map/scatter | solution.py:382
  18.5 1.3 %scatter.30 = f32[160,240]{0,1:T(8,128)S(1)} dynamic-update-slice(f32[160,240]{0,1:T(8,128)S(1)} %scatter.29, f32[40,40]{0,1:T(8,128)S(1)} %get-tuple-element.103, s32[]{:T(128)} %constant.214.clone.1, s32[]{:T(128)} %constant.214.clone.1) | dynamic-update-slice | bytes 12804 | tf_op jit(solution)/shard_map/scatter | solution.py:381
  19.7 1.3 %scatter.31 = f32[160,240]{0,1:T(8,128)S(1)} dynamic-update-slice(f32[160,240]{0,1:T(8,128)S(1)} %scatter.30, f32[40,40]{0,1:T(8,128)S(1)} %copy.22, s32[]{:T(128)} %constant.214.clone.1, s32[]{:T(128)} %constant.215.clone.1) | dynamic-update-slice | bytes 12804 | tf_op jit(solution)/shard_map/scatter | solution.py:382
  21.0 1.3 %scatter.34 = f32[160,240]{0,1:T(8,128)S(1)} dynamic-update-slice(f32[160,240]{0,1:T(8,128)S(1)} %scatter.31, f32[40,40]{0,1:T(8,128)S(1)} %get-tuple-element.104, s32[]{:T(128)} %constant.211.clone.1, s32[]{:T(128)} %constant.211.clone.1) | dynamic-update-slice | bytes 12804 | tf_op jit(solution)/shard_map/scatter | solution.py:381
  22.3 1.3 %scatter.35 = f32[160,240]{0,1:T(8,128)S(1)} dynamic-update-slice(f32[160,240]{0,1:T(8,128)S(1)} %scatter.34, f32[40,40]{0,1:T(8,128)S(1)} %copy.23, s32[]{:T(128)} %constant.211.clone.1, s32[]{:T(128)} %constant.216.clone.1) | dynamic-update-slice | bytes 12804 | tf_op jit(solution)/shard_map/scatter | solution.py:382
  23.6 1.3 %scatter.36 = f32[160,240]{0,1:T(8,128)S(1)} dynamic-update-slice(f32[160,240]{0,1:T(8,128)S(1)} %scatter.35, f32[40,40]{0,1:T(8,128)S(1)} %get-tuple-element.102, s32[]{:T(128)} %constant.215.clone.1, s32[]{:T(128)} %constant.215.clone.1) | dynamic-update-slice | bytes 12804 | tf_op jit(solution)/shard_map/scatter | solution.py:381
  24.9 0.1 copy.24
  25.0 0.9 scatter.39.mix_ref
  25.9 0.0 copy-start
  25.9 0.7 copy-done
  26.6 82.7 %shard_map.113 = (f32[8,256]{1,0:T(8,128)}, f32[2,160,512]{2,1,0:T(8,128)}) custom-call(f32[8,256]{1,0:T(8,128)} %reshape.272.inner_ref, f32[2,160,512]{2,1,0:T(8,128)} %outer_ref.1, f32[8,256]{1,0:T(8,128)} %reshape.273.live_ref, f32[8,256]{1,0:T(8,128)} %reshape.274.energy_ref, f32[1024,2048]{1,0:T(8,128)} %bitcast.27, f32[160,256]{1,0:T(8,128)} %bitcast.28, ...), custom_call_target="tpu_custom_call" | custom-call | tf_op jit(solution)/shard_map/pallas_call | solution.py:386
  109.3 0.7 reshape.282
  110.0 0.6 copy.29
  110.6 2.0 %copy.38 = f32[2,160,512]{2,1,0:T(8,128)} copy(f32[2,160,512]{2,1,0:T(8,128)} %get-tuple-element.113) | data formatting | bytes 1310720
  (5 shorter events, 0.0 us)
Async XLA Ops:
  1.6 12.4 %collective-permute-start = (f32[40,40]{1,0:T(8,128)S(1)}, f32[40,40]{1,0:T(8,128)S(1)}, u32[]{:S(2)}, u32[]{:S(2)}) collective-permute-start(f32[40,40]{1,0:T(8,128)S(1)} %get-tuple-element.107), channel_id=1, source_target_pairs={{0,8},{8,16},{16,24},{1,9},{9,17},{17,25},{2,10},{10,18},{18,26},{... | collective-permute-start | bytes 19208 | tf_op jit(solution)/shard_map/ppermute | solution.py:377
  25.9 0.7 copy-start

commit v2 on v1

--- a/solution.py
+++ b/solution.py
@@ -31,12 +31,13 @@
     ch,
     inner_ref,
     outer_ref,
-    live_ref,
     energy_ref,
     dipole_ref,
     surface_ref,
-    diag_ref,
-    mix_ref,
+    threshold_ref,
+    coef_ref,
+    pattern_ref,
+    size_ref,
     field_ref,
     inner_out,
     outer_out,
@@ -50,7 +51,15 @@
     part_out,
     part_in,
     below_in,
-    mixed,
+    pairs,
+    dip_full,
+    live_ref,
+    energy_rows,
+    total_inner,
+    diag_ref,
+    sem_load,
+    sem_g_send,
+    sem_g_recv,
     sem_a_send,
     sem_a_recv,
     sem_z_send,
@@ -66,8 +75,8 @@
 ):
     z = lax.axis_index("inner")
     me = lax.axis_index("outer")
-    rows, rc = inner_ref.shape
-    blocks = rows // 2
+    blocks, rc = energy_ref.shape
+    rows = 2 * blocks
     nc, nr = outer_ref.shape[1:]
     total = rc * sectors
     width = peer_in.shape[3]
@@ -84,37 +93,133 @@
         above_in[...] = jnp.zeros_like(above_in)
         grid[:, :, ch + nc : 2 * ch + nc, :] = jnp.zeros((2, 2, ch, nr), f32)
 
-    term[...] = inner_ref[...] * live_ref[...]
-    inner_out[...] = term[...]
-    for p in range(2):
+    loads = [
+        pltpu.make_async_copy(
+            dipole_ref.at[pl.ds(l * rc, rc)], dip_full.at[pl.ds(l * rc, rc)], sem_load.at[l]
+        )
+        for l in range(blocks)
+    ]
+    for load in loads:
+        load.start()
+
+    for p in (1, 0):
         x = outer_ref[p]
         grid[0, p, ch : ch + nc, :] = x
         outer_out[p] = x
-    mh, ml = split(mix_ref[...])
-    mix_split[0:nc, :] = mh
-    mix_split[nc : 2 * nc, :] = ml
+
+    def channel_copies(slot, p):
+        up = pltpu.make_async_remote_copy(
+            src_ref=grid.at[slot, p, pl.ds(nc, ch), :],
+            dst_ref=grid.at[slot, p, pl.ds(0, ch), :],
+            send_sem=sem_up_send.at[p],
+            recv_sem=sem_up_recv.at[slot, p],
+            device_id={"inner": z + 1, "outer": me},
+            device_id_type=MESH,
+        )
+        down = pltpu.make_async_remote_copy(
+            src_ref=grid.at[slot, p, pl.ds(ch, ch), :],
+            dst_ref=grid.at[slot, p, pl.ds(ch + nc, ch), :],
+            send_sem=sem_down_send.at[p],
+            recv_sem=sem_down_recv.at[slot, p],
+            device_id={"inner": z - 1, "outer": me},
+            device_id_type=MESH,
+        )
+        return up, down
+
+    side = pairs.shape[1]
+    for l in range(blocks + 1):
+        pairs[l, ch:side, :] = jnp.zeros((side - ch, side), f32)
+    for l in range(blocks):
+        pairs[l + 1, 0:ch, :] = jnp.zeros((ch, side), f32)
+        pairs[l + 1, 0:ch, 0:ch] = coef_ref[l] * pattern_ref[l].astype(f32)
+
+    @pl.when(z == 0)
+    def _():
+        pairs[0, 0:ch, :] = jnp.zeros((ch, side), f32)
+
+    share = pltpu.make_async_remote_copy(
+        src_ref=pairs.at[blocks, pl.ds(0, ch), :],
+        dst_ref=pairs.at[0, pl.ds(0, ch), :],
+        send_sem=sem_g_send,
+        recv_sem=sem_g_recv,
+        device_id={"inner": z + 1, "outer": me},
+        device_id_type=MESH,
+    )
+
+    @pl.when(has_above)
+    def _():
+        share.start()
+        for p in (1, 0):
+            channel_copies(0, p)[0].start()
+
+    @pl.when(has_below)
+    def _():
+        for p in (1, 0):
+            channel_copies(0, p)[1].start()
+
+    order_of = [(l, p) for l in range(blocks) for p in range(2)]
+    position = me * rc + lax.broadcasted_iota(jnp.int32, (1, rc), 1)
+    live_ref[...] = jnp.concatenate(
+        [jnp.where(position < size_ref[l], 1.0, 0.0) for l, p in order_of], axis=0
+    )
+    energy_rows[...] = jnp.concatenate([energy_ref[l : l + 1, :] for l, p in order_of], axis=0)
+    term[...] = live_ref[...] * jnp.concatenate(
+        [inner_ref[p, l : l + 1, :] for l, p in order_of], axis=0
+    )
+    total_inner[...] = term[...]
+
+    eye = lax.broadcasted_iota(jnp.int32, (nc, width), 0) == lax.broadcasted_iota(
+        jnp.int32, (nc, width), 1
+    )
+
+    def to_row(col):
+        return jnp.sum(jnp.where(eye, col, 0.0), axis=0, keepdims=True)
+
+    def to_col(row):
+        return jnp.sum(jnp.where(eye, row, 0.0), axis=1, keepdims=True)
+
+    def wait(ref, sem):
+        pltpu.make_async_copy(ref, ref, sem).wait()
+
+    small = lax.broadcasted_iota(jnp.int32, (nc, nc), 0) == lax.broadcasted_iota(
+        jnp.int32, (nc, nc), 1
+    )
+    diag_ref[...] = 2.0 * kinetic_scale + jnp.sum(
+        jnp.where(small, threshold_ref[...], 0.0), axis=1, keepdims=True
+    )
 
     def split_rows(i, carry):
         at = pl.ds(pl.multiple_of(i * 16, 16), 16)
-        high, low = split(dipole_ref[at, :])
+        high, low = split(dip_full[at, :])
         dip_hi[at, :] = high
         dip_lo[at, :] = low
         return carry
 
-    lax.fori_loop(0, blocks * rc // 16, split_rows, 0)
-
-    eye = lax.broadcasted_iota(jnp.int32, (nc, width), 0) == lax.broadcasted_iota(
-        jnp.int32, (nc, width), 1
-    )
-
-    def to_row(col):
-        return jnp.sum(jnp.where(eye, col, 0.0), axis=0, keepdims=True)
-
-    def to_col(row):
-        return jnp.sum(jnp.where(eye, row, 0.0), axis=1, keepdims=True)
-
-    def wait(ref, sem):
-        pltpu.make_async_copy(ref, ref, sem).wait()
+    for l in range(blocks):
+        loads[l].wait()
+        lax.fori_loop(l * (rc // 16), (l + 1) * (rc // 16), split_rows, 0)
+
+    @pl.when(has_below)
+    def _():
+        share.wait_recv()
+
+    @pl.when(has_above)
+    def _():
+        share.wait_send()
+
+    reach = -(-(nc + 2 * ch) // 128) * 128
+    fill = jnp.zeros((ch, reach - side), f32)
+    mixed_rows = []
+    for l in range(blocks):
+        upward = jnp.concatenate([pairs[l + 1, 0:ch, :], fill], axis=1)
+        downward = jnp.concatenate([pairs[l].T[0:ch], fill], axis=1)
+        upward = pltpu.roll(upward, (l + 2) * ch, 1)
+        if l:
+            downward = pltpu.roll(downward, l * ch, 1)
+        mixed_rows.append((upward + downward)[:, 0 : nc + 2 * ch])
+    mh, ml = split(jnp.concatenate(mixed_rows, axis=0))
+    mix_split[0:nc, :] = mh
+    mix_split[nc : 2 * nc, :] = ml
 
     def apply(t, carry):
         par = lax.rem(t, 2)
@@ -123,23 +228,6 @@
         strength = field_ref[lax.div(t, ORDER)]
         factor = time_step / (order + 1).astype(f32)
         last = order == ORDER - 1
-
-        up = pltpu.make_async_remote_copy(
-            src_ref=grid.at[par, :, pl.ds(nc, ch), :],
-            dst_ref=grid.at[par, :, pl.ds(0, ch), :],
-            send_sem=sem_up_send,
-            recv_sem=sem_up_recv.at[par],
-            device_id={"inner": z + 1, "outer": me},
-            device_id_type=MESH,
-        )
-        down = pltpu.make_async_remote_copy(
-            src_ref=grid.at[par, :, pl.ds(ch, ch), :],
-            dst_ref=grid.at[par, :, pl.ds(ch + nc, ch), :],
-            send_sem=sem_down_send,
-            recv_sem=sem_down_recv.at[par],
-            device_id={"inner": z - 1, "outer": me},
-            device_id_type=MESH,
-        )
 
         c = term[...]
         peer_in[par, me, 0:rows, 0:rc] = c
@@ -162,6 +250,22 @@
         edge_rows.append(jnp.zeros((2, width), f32))
         peer_in[par, me, rows : rows + 8, :] = jnp.concatenate(edge_rows, axis=0)
 
+        @pl.when(has_below)
+        def _():
+            def send_z(s, k):
+                to = lax.rem(me + s, sectors)
+                pltpu.make_async_remote_copy(
+                    src_ref=peer_in.at[par, me, pl.ds(0, 2), pl.ds(0, rc)],
+                    dst_ref=above_in.at[par, me, pl.ds(0, 2)],
+                    send_sem=sem_z_send,
+                    recv_sem=sem_z_recv.at[par],
+                    device_id={"inner": z - 1, "outer": to},
+                    device_id_type=MESH,
+                ).start()
+                return k
+
+            lax.fori_loop(0, sectors, send_z, 0)
+
         def send_a(s, k):
             to = lax.rem(me + s, sectors)
             pltpu.make_async_remote_copy(
@@ -175,23 +279,6 @@
             return k
 
         lax.fori_loop(1, sectors, send_a, 0)
-
-        @pl.when(has_below)
-        def _():
-            def send_z(s, k):
-                to = lax.rem(me + s, sectors)
-                pltpu.make_async_remote_copy(
-                    src_ref=peer_in.at[par, me, pl.ds(0, rows), pl.ds(0, rc)],
-                    dst_ref=above_in.at[par, me],
-                    send_sem=sem_z_send,
-                    recv_sem=sem_z_recv.at[par],
-                    device_id={"inner": z - 1, "outer": to},
-                    device_id_type=MESH,
-                ).start()
-                return k
-
-            lax.fori_loop(0, sectors, send_z, 0)
-            down.start()
 
         row_block = lax.broadcasted_iota(jnp.int32, (rows, 1), 0) // 2
         ch_, cl_ = split(c)
@@ -212,8 +299,8 @@
             def send_y(s, k):
                 to = lax.rem(me + s, sectors)
                 pltpu.make_async_remote_copy(
-                    src_ref=part_out.at[to],
-                    dst_ref=below_in.at[par, me],
+                    src_ref=part_out.at[to, pl.ds(0, 2)],
+                    dst_ref=below_in.at[par, me, pl.ds(0, 2)],
                     send_sem=sem_y_send,
                     recv_sem=sem_y_recv.at[par],
                     device_id={"inner": z + 1, "outer": to},
@@ -222,7 +309,6 @@
                 return k
 
             lax.fori_loop(0, sectors, send_y, 0)
-            up.start()
 
         def send_b(s, k):
             to = lax.rem(me + s, sectors)
@@ -242,7 +328,7 @@
 
         @pl.when(has_above)
         def _():
-            wait(above_in.at[par], sem_z_recv.at[par])
+            wait(above_in.at[par, :, pl.ds(0, 2)], sem_z_recv.at[par])
 
         def forward_rows(values, l):
             vh, vl = values
@@ -279,21 +365,23 @@
             [surf[p][l] for l in range(blocks) for p in range(2)], axis=0
         )
 
-        @pl.when(has_below)
-        def _():
-            wait(grid.at[par, :, pl.ds(0, ch), :], sem_up_recv.at[par])
-
-        @pl.when(has_above)
-        def _():
-            wait(grid.at[par, :, pl.ds(0, ch), :], sem_down_recv.at[par])
-
         bound = jnp.zeros((8, width), f32)
         for k in range(sectors):
             bound = bound + peer_in[par, k, rows : rows + 8, :]
         before = peer_in[par, lax.rem(me + sectors - 1, sectors), rows : rows + 8, :]
         after = peer_in[par, lax.rem(me + 1, sectors), rows : rows + 8, :]
         lane = lax.broadcasted_iota(jnp.int32, (1, nr), 1)
-        for p in range(2):
+        for p in (1, 0):
+            up, down = channel_copies(par, p)
+
+            @pl.when(has_below)
+            def _():
+                up.wait_recv()
+
+            @pl.when(has_above)
+            def _():
+                down.wait_recv()
+
             gh, gl = split(grid[par, p])
             r = lax.dot_general(mix_split[...], gh, NN, preferred_element_type=f32)
             q = lax.dot_general(mix_split[0:nc, :], gl, NN, preferred_element_type=f32)
@@ -310,12 +398,31 @@
             acc = outer_out[1 - p] + value
             outer_out[1 - p] = acc
             grid[nxt, 1 - p, ch : ch + nc, :] = jnp.where(last, acc, value)
+            new_up, new_down = channel_copies(nxt, 1 - p)
+            up_old, down_old = channel_copies(par, 1 - p)
+
+            @pl.when(has_above)
+            def _():
+                up_old.wait_send()
+
+            @pl.when(has_below)
+            def _():
+                down_old.wait_send()
+
+            @pl.when(jnp.logical_and(has_above, t < STEPS * ORDER - 1))
+            def _():
+                new_up.start()
+
+            @pl.when(jnp.logical_and(has_below, t < STEPS * ORDER - 1))
+            def _():
+                new_down.start()
+
 
         wait(part_in.at[par, pl.ds(0, sectors - 1)], sem_b_recv.at[par])
 
         @pl.when(has_below)
         def _():
-            wait(below_in.at[par], sem_y_recv.at[par])
+            wait(below_in.at[par, :, pl.ds(0, 2)], sem_y_recv.at[par])
 
         near = part_in[par, 0]
         far = below_in[par, 0]
@@ -324,14 +431,14 @@
             far = far + below_in[par, k]
         behind = jnp.where(row_block == 0, far, near)
         image = live_ref[...] * (
-            energy_ref[...] * c + strength * (ahead + behind) - kinetic_scale * surf
+            energy_rows[...] * c + strength * (ahead + behind) - kinetic_scale * surf
         )
         even = lax.rem(lax.broadcasted_iota(jnp.int32, (rows, 1), 0), 2) == 0
         value = factor * jnp.where(
             even, pltpu.roll(image, rows - 1, 0), -pltpu.roll(image, 1, 0)
         )
-        acc = inner_out[...] + value
-        inner_out[...] = acc
+        acc = total_inner[...] + value
+        total_inner[...] = acc
         term[...] = jnp.where(last, acc, value)
 
         wait(peer_in.at[par, pl.ds(0, sectors - 1)], sem_a_send)
@@ -339,17 +446,20 @@
 
         @pl.when(has_below)
         def _():
-            wait(above_in.at[par], sem_z_send)
-            down.wait_send()
+            wait(above_in.at[par, :, pl.ds(0, 2)], sem_z_send)
 
         @pl.when(has_above)
         def _():
-            wait(below_in.at[par], sem_y_send)
-            up.wait_send()
+            wait(below_in.at[par, :, pl.ds(0, 2)], sem_y_send)
 
         return carry
 
     lax.fori_loop(0, STEPS * ORDER, apply, 0)
+    final = total_inner[...]
+    for p in range(2):
+        inner_out[p] = jnp.concatenate(
+            [final[2 * l + p : 2 * l + p + 1] for l in range(blocks)], axis=0
+        )
 
 
 def local(
@@ -371,25 +481,20 @@
     nc, nr = outer_state.shape[1:]
     rows = 2 * blocks
     width = max(rc, -(-nc // 128) * 128)
-    row_index = lax.axis_index("outer") * rc + jnp.arange(rc, dtype=jnp.int32)
-    live = (row_index[None, :] < block_sizes[:, None]).astype(f32)
-    coupling = coupling_coef * coupling_pattern.astype(f32)
-    below = lax.ppermute(coupling[blocks - 1], "inner", [(i, i + 1) for i in range(planes - 1)])
-    mix = jnp.zeros((nc, nc + 2 * ch), f32)
-    for l in range(blocks):
-        source = below if l == 0 else coupling[l - 1]
-        mix = mix.at[l * ch : (l + 1) * ch, l * ch : (l + 1) * ch].set(source.T)
-        mix = mix.at[l * ch : (l + 1) * ch, (l + 2) * ch : (l + 3) * ch].set(coupling[l])
-    diag = (thresholds + 2.0 * kinetic_scale)[:, None]
     vmem = pl.BlockSpec(memory_space=pltpu.VMEM)
     dma = pltpu.SemaphoreType.DMA
-    inner_final, outer_final = pl.pallas_call(
+    smem = pl.BlockSpec(memory_space=pltpu.SMEM)
+    side = -(-ch // 128) * 128
+    return pl.pallas_call(
         functools.partial(kernel, planes, sectors, ch),
         out_shape=(
-            jax.ShapeDtypeStruct((rows, rc), f32),
+            jax.ShapeDtypeStruct((2, blocks, rc), f32),
             jax.ShapeDtypeStruct((2, nc, nr), f32),
         ),
-        in_specs=[vmem] * 8 + [pl.BlockSpec(memory_space=pltpu.SMEM)],
+        in_specs=[vmem] * 3
+        + [pl.BlockSpec(memory_space=pltpu.HBM)]
+        + [vmem] * 4
+        + [smem] * 2,
         out_specs=(vmem, vmem),
         scratch_shapes=[
             pltpu.VMEM((blocks * rc, total), bf16),
@@ -402,26 +507,32 @@
             pltpu.VMEM((sectors, rows, rc), f32),
             pltpu.VMEM((2, sectors, rows, rc), f32),
             pltpu.VMEM((2, sectors, rows, rc), f32),
-            pltpu.VMEM((8, 128), f32),
+            pltpu.VMEM((blocks + 1, side, side), f32),
+            pltpu.VMEM((blocks * rc, total), f32),
+            pltpu.VMEM((rows, rc), f32),
+            pltpu.VMEM((rows, rc), f32),
+            pltpu.VMEM((rows, rc), f32),
+            pltpu.VMEM((nc, 1), f32),
+            dma((blocks,)), dma(()), dma(()),
             dma(()), dma((2,)), dma(()), dma((2,)),
             dma(()), dma((2,)), dma(()), dma((2,)),
-            dma(()), dma((2,)), dma(()), dma((2,)),
+            dma((2,)), dma((2, 2)), dma((2,)), dma((2, 2)),
         ],
         compiler_params=pltpu.CompilerParams(
             has_side_effects=True, vmem_limit_bytes=56 * 1024 * 1024
         ),
     )(
-        inner_state.transpose(1, 0, 2).reshape(rows, rc),
+        inner_state,
         outer_state,
-        jnp.repeat(live, 2, axis=0),
-        jnp.repeat(energies, 2, axis=0),
+        energies,
         dipole.reshape(blocks * rc, total),
         surface.reshape(nc, rc),
-        diag,
-        mix,
+        thresholds.reshape(1, nc),
+        coupling_coef,
+        coupling_pattern,
+        block_sizes,
         field_strength,
     )
-    return inner_final.reshape(blocks, 2, rc).transpose(1, 0, 2), outer_final
 
 
 def solution(mesh):

time: 113 us -> 87.5 us (0.77)
  local copies, waits for them, and re-layouts: 19.9 us -> 3.26 us
  starting transfers between devices: 4.96 us -> 0 us
  other arithmetic: 4.3 us -> 0 us
    scatter x9 -> x0, local copies, waits for them, and re-layouts: 9.71 us -> none  [the longest x4 5.73 us: local(): mix.at[l * ch:(l + 1) * ch, (l + 2) * ch:(l + 3) * ch].set(coupling[l])]
    ppermute x1 -> x0, starting transfers between devices: 4.96 us -> none  [local(): lax.ppermute(coupling[blocks - 1], 'inner', [(i, i + 1) for i in range(pl...]
    reshape x5 -> x0, local copies, waits for them, and re-layouts: 3.13 us -> none  [the longest x2 1.31 us: local(): return (inner_final.reshape(blocks, 2, rc).transpose(1, 0, 2), outer_final)]
    another operation x6 -> x0, local copies, waits for them, and re-layouts: 2.19 us -> none
    another operation x3 -> x0, other arithmetic: 1.95 us -> none
    broadcast_in_dim x3 -> x0, local copies, waits for them, and re-layouts: 1.44 us -> none  [the longest x1 0.74 us: local(): diag = (thresholds + 2.0 * kinetic_scale)[:, None]]
    unnamed x4 -> x2, local copies, waits for them, and re-layouts: 2.7 us -> 3.26 us
  transfers between devices with their start and end apart: 1 -> 0, of which waited for: 0 -> 0; matrix products, arithmetic and copies ran while one was open for 7% -> 0% of each run, Pallas kernels for 0% -> 0%
where the time goes in v2:
time: 87.5 us; the launch traced here: 87.2 us
  Pallas kernels  83.3 us (95%)
  local copies, waits for them, and re-layouts  3.26 us (4%)
    pallas_call x1, Pallas kernels, local(): pl.pallas_call(functools.partial(kernel, planes, sectors, ch), out_shape=...  83.3 us
    unnamed x2, local copies, waits for them, and re-layouts  3.26 us

profile of v2, /device:TPU:0, one launch (start us, length us, event | category | flops | bytes accessed | tf_op | source)
XLA Modules:
  0.0 87.2 jit_solution(4416437161688758012)
XLA Ops:
  0.6 83.3 %shard_map.113 = (f32[2,4,256]{2,1,0:T(4,128)}, f32[2,160,512]{2,1,0:T(8,128)}) custom-call(f32[2,4,256]{2,1,0:T(4,128)} %inner_ref.1, f32[2,160,512]{2,1,0:T(8,128)} %outer_ref.1, f32[4,256]{1,0:T(4,128)} %energy_ref.1, f32[1024,2048]{1,0:T(8,128)} %bitcast.3, f32[160,256]{1,0:T(8,128)} %bitcast.4, f32[1,160]{1,0:T(1,128)} %bitcast.5, ...), custom_call_target="tpu_custom_call" | custom-call | tf_op jit(solution)/shard_map/pallas_call | solution.py:488
  84.0 1.3 %copy.14 = f32[2,4,256]{2,1,0:T(4,128)} copy(f32[2,4,256]{2,1,0:T(4,128)} %get-tuple-element.4) | data formatting | bytes 16384
  85.3 2.0 %copy.15 = f32[2,160,512]{2,1,0:T(8,128)} copy(f32[2,160,512]{2,1,0:T(8,128)} %get-tuple-element.5) | data formatting | bytes 1310720

commit v3 on v2

--- a/solution.py
+++ b/solution.py
@@ -57,6 +57,9 @@
     energy_rows,
     total_inner,
     diag_ref,
+    edge_in,
+    sem_e_send,
+    sem_e_recv,
     sem_load,
     sem_g_send,
     sem_g_recv,
@@ -79,7 +82,7 @@
     rows = 2 * blocks
     nc, nr = outer_ref.shape[1:]
     total = rc * sectors
-    width = peer_in.shape[3]
+    width = edge_in.shape[3]
     has_below = z > 0
     has_above = z < planes - 1
 
@@ -231,6 +234,36 @@
 
         c = term[...]
         peer_in[par, me, 0:rows, 0:rc] = c
+        def send_a(s, k):
+            to = lax.rem(me + s, sectors)
+            pltpu.make_async_remote_copy(
+                src_ref=peer_in.at[par, me],
+                dst_ref=peer_in.at[par, me],
+                send_sem=sem_a_send,
+                recv_sem=sem_a_recv.at[par],
+                device_id={"inner": z, "outer": to},
+                device_id_type=MESH,
+            ).start()
+            return k
+
+        lax.fori_loop(1, sectors, send_a, 0)
+
+        @pl.when(has_below)
+        def _():
+            def send_z(s, k):
+                to = lax.rem(me + s, sectors)
+                pltpu.make_async_remote_copy(
+                    src_ref=peer_in.at[par, me, pl.ds(0, 2), pl.ds(0, rc)],
+                    dst_ref=above_in.at[par, me, pl.ds(0, 2)],
+                    send_sem=sem_z_send,
+                    recv_sem=sem_z_recv.at[par],
+                    device_id={"inner": z - 1, "outer": to},
+                    device_id_type=MESH,
+                ).start()
+                return k
+
+            lax.fori_loop(0, sectors, send_z, 0)
+
         edge_rows = []
         for p in range(2):
             edge_rows.append(to_row(grid[par, p, ch : ch + nc, 0:1]))
@@ -248,37 +281,31 @@
                 to_row(jnp.sum(surface_ref[...] * spread, axis=1, keepdims=True))
             )
         edge_rows.append(jnp.zeros((2, width), f32))
-        peer_in[par, me, rows : rows + 8, :] = jnp.concatenate(edge_rows, axis=0)
-
-        @pl.when(has_below)
-        def _():
-            def send_z(s, k):
-                to = lax.rem(me + s, sectors)
-                pltpu.make_async_remote_copy(
-                    src_ref=peer_in.at[par, me, pl.ds(0, 2), pl.ds(0, rc)],
-                    dst_ref=above_in.at[par, me, pl.ds(0, 2)],
-                    send_sem=sem_z_send,
-                    recv_sem=sem_z_recv.at[par],
-                    device_id={"inner": z - 1, "outer": to},
-                    device_id_type=MESH,
-                ).start()
-                return k
-
-            lax.fori_loop(0, sectors, send_z, 0)
-
-        def send_a(s, k):
+        edge_in[par, me] = jnp.concatenate(edge_rows, axis=0)
+
+        def edge_copy(s):
             to = lax.rem(me + s, sectors)
-            pltpu.make_async_remote_copy(
-                src_ref=peer_in.at[par, me],
-                dst_ref=peer_in.at[par, me],
-                send_sem=sem_a_send,
-                recv_sem=sem_a_recv.at[par],
+            need = (s == 1) | (s == sectors - 1) | (to == 0) | (me == 0)
+            out = pltpu.make_async_remote_copy(
+                src_ref=edge_in.at[par, me],
+                dst_ref=edge_in.at[par, me],
+                send_sem=sem_e_send.at[to],
+                recv_sem=sem_e_recv.at[par, me],
                 device_id={"inner": z, "outer": to},
                 device_id_type=MESH,
-            ).start()
+            )
+            return need, to, out
+
+        def send_e(s, k):
+            need, to, out = edge_copy(s)
+
+            @pl.when(need)
+            def _():
+                out.start()
+
             return k
 
-        lax.fori_loop(1, sectors, send_a, 0)
+        lax.fori_loop(1, sectors, send_e, 0)
 
         row_block = lax.broadcasted_iota(jnp.int32, (rows, 1), 0) // 2
         ch_, cl_ = split(c)
@@ -326,10 +353,6 @@
 
         wait(peer_in.at[par, pl.ds(0, sectors - 1)], sem_a_recv.at[par])
 
-        @pl.when(has_above)
-        def _():
-            wait(above_in.at[par, :, pl.ds(0, 2)], sem_z_recv.at[par])
-
         def forward_rows(values, l):
             vh, vl = values
             at = pl.ds(l * rc, rc)
@@ -342,17 +365,32 @@
         own = split(
             jnp.concatenate([peer_in[par, k, 0:rows, 0:rc] for k in range(sectors)], axis=1)
         )
+        ahead = jnp.zeros((rows, rc), f32)
+        for l in range(blocks - 1):
+            ahead = jnp.where(row_block == l + 1, forward_rows(own, l), ahead)
+
+        @pl.when(has_above)
+        def _():
+            wait(above_in.at[par, :, pl.ds(0, 2)], sem_z_recv.at[par])
+
         other = split(jnp.concatenate([above_in[par, k] for k in range(sectors)], axis=1))
-        ahead = jnp.zeros((rows, rc), f32)
-        for l in range(blocks):
-            if l < blocks - 1:
-                ahead = jnp.where(row_block == l + 1, forward_rows(own, l), ahead)
-            else:
-                ahead = jnp.where(row_block == 0, forward_rows(other, l), ahead)
+        ahead = jnp.where(row_block == 0, forward_rows(other, blocks - 1), ahead)
         ahead = pltpu.roll(ahead, rows - 2, 0)
 
+        def take_e(s, k):
+            need, source, out = edge_copy(s)
+
+            @pl.when(need)
+            def _():
+                wait(edge_in.at[par, source], sem_e_recv.at[par, source])
+                out.wait_send()
+
+            return k
+
+        lax.fori_loop(1, sectors, take_e, 0)
+
         surf = []
-        edge = peer_in[par, 0, rows : rows + 8, :]
+        edge = edge_in[par, 0]
         for p in range(2):
             prod = surface_ref[...] * to_col(edge[p : p + 1])
             surf.append(
@@ -367,9 +405,9 @@
 
         bound = jnp.zeros((8, width), f32)
         for k in range(sectors):
-            bound = bound + peer_in[par, k, rows : rows + 8, :]
-        before = peer_in[par, lax.rem(me + sectors - 1, sectors), rows : rows + 8, :]
-        after = peer_in[par, lax.rem(me + 1, sectors), rows : rows + 8, :]
+            bound = bound + edge_in[par, k]
+        before = edge_in[par, lax.rem(me + sectors - 1, sectors)]
+        after = edge_in[par, lax.rem(me + 1, sectors)]
         lane = lax.broadcasted_iota(jnp.int32, (1, nr), 1)
         for p in (1, 0):
             up, down = channel_copies(par, p)
@@ -502,7 +540,7 @@
             pltpu.VMEM((2 * nc, nc + 2 * ch), bf16),
             pltpu.VMEM((2, 2, nc + 2 * ch, nr), f32),
             pltpu.VMEM((rows, rc), f32),
-            pltpu.VMEM((2, sectors, rows + 8, width), f32),
+            pltpu.VMEM((2, sectors, rows, rc), f32),
             pltpu.VMEM((2, sectors, rows, rc), f32),
             pltpu.VMEM((sectors, rows, rc), f32),
             pltpu.VMEM((2, sectors, rows, rc), f32),
@@ -513,6 +551,8 @@
             pltpu.VMEM((rows, rc), f32),
             pltpu.VMEM((rows, rc), f32),
             pltpu.VMEM((nc, 1), f32),
+            pltpu.VMEM((2, sectors, 8, width), f32),
+            dma((sectors,)), dma((2, sectors)),
             dma((blocks,)), dma(()), dma(()),
             dma(()), dma((2,)), dma(()), dma((2,)),
             dma(()), dma((2,)), dma(()), dma((2,)),

time: 87.5 us -> 79.7 us (0.911)
  Pallas kernels: 83.3 us -> 75.5 us
    pallas_call x1, Pallas kernels: 83.3 us -> 75.5 us  [local(): pl.pallas_call(functools.partial(kernel, planes, sectors, ch), out_shape=...]
where the time goes in v3:
time: 79.7 us; the launch traced here: 79.4 us
  Pallas kernels  75.5 us (95%)
  local copies, waits for them, and re-layouts  3.26 us (4%)
    pallas_call x1, Pallas kernels, local(): pl.pallas_call(functools.partial(kernel, planes, sectors, ch), out_shape=...  75.5 us
    unnamed x2, local copies, waits for them, and re-layouts  3.26 us

profile of v3, /device:TPU:0, one launch (start us, length us, event | category | flops | bytes accessed | tf_op | source)
XLA Modules:
  0.0 79.4 jit_solution(1823971366774465261)
XLA Ops:
  0.6 75.5 %shard_map.113 = (f32[2,4,256]{2,1,0:T(4,128)}, f32[2,160,512]{2,1,0:T(8,128)}) custom-call(f32[2,4,256]{2,1,0:T(4,128)} %inner_ref.1, f32[2,160,512]{2,1,0:T(8,128)} %outer_ref.1, f32[4,256]{1,0:T(4,128)} %energy_ref.1, f32[1024,2048]{1,0:T(8,128)} %bitcast.3, f32[160,256]{1,0:T(8,128)} %bitcast.4, f32[1,160]{1,0:T(1,128)} %bitcast.5, ...), custom_call_target="tpu_custom_call" | custom-call | tf_op jit(solution)/shard_map/pallas_call | solution.py:526
  76.2 1.3 %copy.14 = f32[2,4,256]{2,1,0:T(4,128)} copy(f32[2,4,256]{2,1,0:T(4,128)} %get-tuple-element.4) | data formatting | bytes 16384
  77.5 2.0 %copy.15 = f32[2,160,512]{2,1,0:T(8,128)} copy(f32[2,160,512]{2,1,0:T(8,128)} %get-tuple-element.5) | data formatting | bytes 1310720
